TPU v7x, 256 devices: a whole 4x4x8 slice. The times are simulated.
256 devices in a mesh: section: 8 (over y, x_hi), dp: 32 (over z, x_lo, core).
Axes of the slice: x: 4 (x_hi: 2, x_lo: 2; x = x_hi * 2 + x_lo), y: 4, z: 8, core: 2. Of those that a mesh axis runs over, the one named last changes fastest.
Arguments:
- block_inputs: bfloat16 [8, 4, 2048, 2048], P('section', None, 'dp'), may hold values from -6 to 6
- mixed_inputs: bfloat16 [8, 4, 2048, 2048], P('section', None, 'dp'), may hold values from -6 to 6
- token_ids: int32 [4, 2048], P(None, 'dp'), may hold values from 0 to 2047
- target_ids: int32 [4, 2048], P(None, 'dp'), may hold values from 0 to 2047
- final_gain: float32 [2048], replicated, may hold values from 0.5 to 1.5
- out_weight: bfloat16 [8, 2048, 2048], P('section'), may hold values from -0.046875 to 0.046875
- head_weight: bfloat16 [2048, 2048], P('section'), may hold values from -0.375 to 0.375
- out_master: float32 [8, 2048, 2048], P('section', 'dp'), may hold values from -0.125 to 0.125
- out_first: float32 [8, 2048, 2048], P('section', 'dp'), may hold values from -2.5 to 2.5
- out_second: float32 [8, 2048, 2048], P('section', 'dp'), may hold values from 4 to 80
- head_master: float32 [2048, 2048], P(('section', 'dp')), may hold values from -0.125 to 0.125
- head_first: float32 [2048, 2048], P(('section', 'dp')), may hold values from -1.5 to 1.5
- head_second: float32 [2048, 2048], P(('section', 'dp')), may hold values from 1.2 to 24
- embed_master: float32 [2048, 2048], P(('section', 'dp')), may hold values from -0.125 to 0.125
- embed_first: float32 [2048, 2048], P(('section', 'dp')), may hold values from -0.125 to 0.125
- embed_second: float32 [2048, 2048], P(('section', 'dp')), may hold values from 0.009765625 to 0.1953125
Outputs:
- out_master_next: float32 [8, 2048, 2048], P('section', 'dp')
- out_first_next: float32 [8, 2048, 2048], P('section', 'dp')
- out_second_next: float32 [8, 2048, 2048], P('section', 'dp')
- head_master_next: float32 [2048, 2048], P(('section', 'dp'))
- head_first_next: float32 [2048, 2048], P(('section', 'dp'))
- head_second_next: float32 [2048, 2048], P(('section', 'dp'))
- embed_master_next: float32 [2048, 2048], P(('section', 'dp'))
- embed_first_next: float32 [2048, 2048], P(('section', 'dp'))
- embed_second_next: float32 [2048, 2048], P(('section', 'dp'))
Inputs may be any that keep to these rules, and one draw needn't show every extreme that they name: `token_ids`: every token id lies in 0 to 2047. `target_ids`: every target id lies in 0 to 2047.
All inputs are finite; a program needn't handle non-finite values.
Results may differ from a plain program's by a relative error of at most 0.00155.
Values may be sent and summed in bfloat16 or wider, within the bound.
A program may use at most 128 MiB of HBM per device.

v0:
```python
import jax
import jax.numpy as jnp
from jax import lax
from jax.sharding import PartitionSpec as P

norm_eps = 1e-05
beta_first = 0.9
beta_second = 0.95
adam_eps = 1e-05
learning_rate = 0.0003
decay_rate = 0.1


def broadcast(value, axis, source):
    kept = jnp.where(lax.axis_index(axis) == source, value, 0).astype(value.dtype)
    return lax.psum(kept, axis)


def shifted_2(value, axis, steps):
    count = lax.axis_size(axis)
    leading, last = max(0, -steps), min(count, count - steps)
    return lax.ppermute(value, axis, [(source, source + steps) for source in range(leading, last)])


def times_transposed(former, latter):
    return lax.dot_general(
        former, latter, (((1,), (1,)), ((), ())), preferred_element_type=jnp.float32
    )


def transposed_times(former, latter):
    return lax.dot_general(
        former, latter, (((0,), (0,)), ((), ())), preferred_element_type=jnp.float32
    )


def plain_times(former, latter):
    return jnp.dot(former, latter, preferred_element_type=jnp.float32)


def normalize(values, gain):
    inverse = lax.rsqrt(jnp.mean(values * values, axis=-1, keepdims=True) + norm_eps)
    return (inverse, values * inverse * gain)


def norm_backward(values, inverse, scaled_cotangent):
    unit = values * inverse
    return inverse * (
        scaled_cotangent - unit * jnp.mean(scaled_cotangent * unit, axis=-1, keepdims=True)
    )


def adam_update(master, first, second, gradient):
    first_next = beta_first * first + (1.0 - beta_first) * gradient
    second_next = beta_second * second + (1.0 - beta_second) * gradient * gradient
    master_next = master - learning_rate * (
        first_next / (jnp.sqrt(second_next) + adam_eps) + decay_rate * master
    )
    return (master_next, first_next, second_next)


def per_device(
    block_inputs,
    mixed_inputs,
    token_ids,
    target_ids,
    final_gain,
    out_weight,
    head_weight,
    out_master,
    out_first,
    out_second,
    head_master,
    head_first,
    head_second,
    embed_master,
    embed_first,
    embed_second,
):
    sections = lax.axis_size("section")
    section = lax.axis_index("section")
    last = sections - 1
    batches, rows, width = mixed_inputs[0].shape
    flat_mixed = mixed_inputs[0].reshape(batches * rows, width)
    wide = block_inputs[0].reshape(batches * rows, width).astype(jnp.float32)
    slice_rows = head_weight.shape[0]
    vocabulary_start = section * slice_rows
    columns = vocabulary_start + lax.broadcasted_iota(jnp.int32, (1, slice_rows), 1)
    final = wide + times_transposed(flat_mixed, out_weight[0])
    final_inverse, final_scaled = normalize(final, final_gain)
    shared_hidden = broadcast(final_scaled.astype(jnp.bfloat16), "section", last)
    logits = times_transposed(shared_hidden, head_weight)
    local_top = jnp.max(logits, axis=1)
    row_top = lax.pmax(local_top, "section")
    shifted = jnp.exp(logits - row_top[:, None])
    row_total = lax.psum(jnp.sum(shifted, axis=1), "section")
    predicted = shifted / row_total[:, None]
    target_flat = target_ids.reshape(-1)
    logit_cotangent = jnp.where(target_flat[:, None] == columns, predicted - 1.0, predicted).astype(
        jnp.bfloat16
    )
    hidden_cotangent = lax.psum(plain_times(logit_cotangent, head_weight), "section")
    top_cotangent = norm_backward(final, final_inverse, hidden_cotangent * final_gain).astype(
        jnp.bfloat16
    )

    def reduce_head():

        def head_term(count):
            part = lax.slice_in_dim(logit_cotangent, 0, count, axis=1)
            return transposed_times(part, shared_hidden)

        return lax.psum_scatter(
            head_term(lax.axis_size("dp") * head_master.shape[0]),
            "dp",
            scatter_dimension=0,
            tiled=True,
        )

    def relay(step, held):
        received = shifted_2(held, "section", -1)
        return jnp.where(section == last, held, received)

    cotangent = lax.fori_loop(0, last, relay, top_cotangent)
    out_term = transposed_times(cotangent, flat_mixed)
    out_gradient = lax.psum_scatter(out_term, "dp", scatter_dimension=0, tiled=True)
    tokens_flat = token_ids.reshape(-1)

    def embed_term(count):
        wanted = vocabulary_start + lax.broadcasted_iota(jnp.int32, (1, count), 1)
        marks = (tokens_flat[:, None] == wanted).astype(jnp.bfloat16)
        return transposed_times(marks, cotangent)

    embed_gradient = lax.psum_scatter(
        embed_term(lax.axis_size("dp") * embed_master.shape[0]),
        "dp",
        scatter_dimension=0,
        tiled=True,
    )
    head_gradient = reduce_head()
    out_out = adam_update(out_master, out_first, out_second, out_gradient.reshape(out_master.shape))
    head_out = adam_update(head_master, head_first, head_second, head_gradient)
    embed_out = adam_update(embed_master, embed_first, embed_second, embed_gradient)
    return (
        out_out[0],
        out_out[1],
        out_out[2],
        head_out[0],
        head_out[1],
        head_out[2],
        embed_out[0],
        embed_out[1],
        embed_out[2],
    )


def solution(mesh):
    in_specs = (
        P("section", None, "dp", None),
        P("section", None, "dp", None),
        P(None, "dp"),
        P(None, "dp"),
        P(),
        P("section", None, None),
        P("section", None),
        P("section", "dp", None),
        P("section", "dp", None),
        P("section", "dp", None),
        P(("section", "dp"), None),
        P(("section", "dp"), None),
        P(("section", "dp"), None),
        P(("section", "dp"), None),
        P(("section", "dp"), None),
        P(("section", "dp"), None),
    )
    out_specs = (
        P("section", "dp", None),
        P("section", "dp", None),
        P("section", "dp", None),
        P(("section", "dp"), None),
        P(("section", "dp"), None),
        P(("section", "dp"), None),
        P(("section", "dp"), None),
        P(("section", "dp"), None),
        P(("section", "dp"), None),
    )
    return jax.shard_map(
        per_device, mesh=mesh, in_specs=in_specs, out_specs=out_specs, check_vma=False
    )
```

profile of v0, /device:TPU:7, one launch (start us, length us, event | category | flops | bytes accessed | tf_op | source)
XLA Modules:
  0.0 794.1 jit_solution(14796199618525828025)
XLA Ops:
  7.2 0.0 copy-start
  7.2 0.0 all-reduce.3.cloned.1.call-start
  7.2 1.2 copy-done
  8.4 6.1 multiply_reduce_fusion.1
  14.6 0.0 copy-start.13
  14.6 1.5 fusion.5
  16.1 0.0 all-reduce.3.cloned.1.call-update
  16.1 0.0 all-reduce.5.cloned.1.call-start
  16.2 0.1 eq.34
  16.3 91.2 %all-reduce.3.cloned.1.call-done = bf16[256,2048]{1,0:T(8,128)(2,1)} async-done(((bf16[256,2048]{1,0:T(8,128)(2,1)}), bf16[256,2048]{1,0:T(8,128)(2,1)}) %all-reduce.3.cloned.1.call-update) | async-done | bytes 1048592 | tf_op jit(solution)/shard_map/psum | solution.py:16
  107.4 2.0 fusion.23
  109.4 18.0 %pmax.7 = f32[256]{0:T(256)S(1)} all-reduce(f32[256]{0:T(256)S(1)} %get-tuple-element.66), channel_id=1, replica_groups=mesh['section'=8,'dp'=32] {'section'}, use_global_device_ids=true, to_apply=%region_3.4 | all-reduce | flops 256 | bytes 2048 | tf_op jit(solution)/shard_map/pmax | solution.py:94
  127.5 0.1 fusion.11
  127.6 18.1 %psum.22 = f32[256]{0:T(256)S(1)} all-reduce(f32[256]{0:T(256)S(1)} %fusion.11), channel_id=1, replica_groups=mesh['section'=8,'dp'=32] {'section'}, use_global_device_ids=true, to_apply=%region_5.6 | all-reduce | flops 256 | bytes 2048 | tf_op jit(solution)/shard_map/psum | solution.py:96
  145.7 3.1 fusion.18
  148.8 0.0 all-reduce.5.cloned.1.call-update
  148.8 0.0 reduce-scatter.6.cloned.1.call-start
  148.9 0.1 eq.39
  149.0 3.0 fusion.16
  152.0 0.0 reduce-scatter.6.cloned.1.call-update
  152.0 0.0 reduce-scatter.8.cloned.1.call-start
  152.1 117.4 %all-reduce.5.cloned.1.call-done = f32[256,2048]{1,0:T(8,128)} async-done(((f32[256,2048]{1,0:T(8,128)}), f32[256,2048]{1,0:T(8,128)}) %all-reduce.5.cloned.1.call-update) | async-done | bytes 2097168 | tf_op jit(solution)/shard_map/psum | solution.py:102
  269.5 2.1 multiply_reduce_fusion
  271.7 0.1 copy-done.2
  271.7 2.1 multiply_convert_fusion
  273.8 191.2 %while.12 = (s32[]{:T(128)}, bf16[256,2048]{1,0:T(8,128)(2,1)S(1)}, pred[]{:T(512)}, s32[]{:T(128)}) while((s32[]{:T(128)}, bf16[256,2048]{1,0:T(8,128)(2,1)S(1)}, pred[]{:T(512)}, s32[]{:T(128)}) %tuple.37), condition=%wide.region_9.10_spmd, body=%wide.region_8.9_spmd.sunk | while | flops 524290 | bytes 7340126 | solution.py:124
  273.8 4.3 collective-permute-start
  278.1 27.8 %collective-permute-done = bf16[256,2048]{1,0:T(8,128)(2,1)S(1)} collective-permute-done((bf16[256,2048]{1,0:T(8,128)(2,1)S(1)}, bf16[256,2048]{1,0:T(8,128)(2,1)S(1)}, u32[]{:S(2)}, u32[]{:S(2)}) %collective-permute-start) | collective-permute-done | bytes 1048608 | tf_op jit(solution)/shard_map/while/body/eval_jaxpr/ppermute | solution.py:22
  305.9 0.3 broadcast_select_fusion.2
  306.2 2.7 collective-permute-start
  308.9 28.1 %collective-permute-done = bf16[256,2048]{1,0:T(8,128)(2,1)S(1)} collective-permute-done((bf16[256,2048]{1,0:T(8,128)(2,1)S(1)}, bf16[256,2048]{1,0:T(8,128)(2,1)S(1)}, u32[]{:S(2)}, u32[]{:S(2)}) %collective-permute-start) | collective-permute-done | bytes 1048608 | tf_op jit(solution)/shard_map/while/body/eval_jaxpr/ppermute | solution.py:22
  336.9 0.3 broadcast_select_fusion.2
  337.2 2.6 collective-permute-start
  339.8 28.2 %collective-permute-done = bf16[256,2048]{1,0:T(8,128)(2,1)S(1)} collective-permute-done((bf16[256,2048]{1,0:T(8,128)(2,1)S(1)}, bf16[256,2048]{1,0:T(8,128)(2,1)S(1)}, u32[]{:S(2)}, u32[]{:S(2)}) %collective-permute-start) | collective-permute-done | bytes 1048608 | tf_op jit(solution)/shard_map/while/body/eval_jaxpr/ppermute | solution.py:22
  368.0 0.3 broadcast_select_fusion.2
  368.2 1.9 collective-permute-start
  370.2 25.8 %collective-permute-done = bf16[256,2048]{1,0:T(8,128)(2,1)S(1)} collective-permute-done((bf16[256,2048]{1,0:T(8,128)(2,1)S(1)}, bf16[256,2048]{1,0:T(8,128)(2,1)S(1)}, u32[]{:S(2)}, u32[]{:S(2)}) %collective-permute-start) | collective-permute-done | bytes 1048608 | tf_op jit(solution)/shard_map/while/body/eval_jaxpr/ppermute | solution.py:22
  396.0 0.3 broadcast_select_fusion.2
  396.3 2.9 collective-permute-start
  399.1 20.3 %collective-permute-done = bf16[256,2048]{1,0:T(8,128)(2,1)S(1)} collective-permute-done((bf16[256,2048]{1,0:T(8,128)(2,1)S(1)}, bf16[256,2048]{1,0:T(8,128)(2,1)S(1)}, u32[]{:S(2)}, u32[]{:S(2)}) %collective-permute-start) | collective-permute-done | bytes 1048608 | tf_op jit(solution)/shard_map/while/body/eval_jaxpr/ppermute | solution.py:22
  419.5 0.3 broadcast_select_fusion.2
  419.8 2.7 collective-permute-start
  422.5 19.0 %collective-permute-done = bf16[256,2048]{1,0:T(8,128)(2,1)S(1)} collective-permute-done((bf16[256,2048]{1,0:T(8,128)(2,1)S(1)}, bf16[256,2048]{1,0:T(8,128)(2,1)S(1)}, u32[]{:S(2)}, u32[]{:S(2)}) %collective-permute-start) | collective-permute-done | bytes 1048608 | tf_op jit(solution)/shard_map/while/body/eval_jaxpr/ppermute | solution.py:22
  441.5 0.3 broadcast_select_fusion.2
  441.8 2.8 collective-permute-start
  444.6 20.1 %collective-permute-done = bf16[256,2048]{1,0:T(8,128)(2,1)S(1)} collective-permute-done((bf16[256,2048]{1,0:T(8,128)(2,1)S(1)}, bf16[256,2048]{1,0:T(8,128)(2,1)S(1)}, u32[]{:S(2)}, u32[]{:S(2)}) %collective-permute-start) | collective-permute-done | bytes 1048608 | tf_op jit(solution)/shard_map/while/body/eval_jaxpr/ppermute | solution.py:22
  464.7 0.3 broadcast_select_fusion.2
  465.0 1.8 fusion.9
  466.7 0.0 reduce-scatter.8.cloned.1.call-update
  466.8 0.0 reduce-scatter.4.cloned.1.call-start
  466.8 8.1 %fusion.24 = f32[2048,2048]{1,0:T(8,128)} fusion(bf16[256,2048]{1,0:T(8,128)(2,1)S(1)} %get-tuple-element.48, bf16[256,2048]{1,0:T(8,128)(2,1)S(1)} %bitcast.27), kind=kOutput, calls=%fused_computation.36 | convolution fusion | flops 2147483648 | bytes 18874368 | tf_op jit(solution)/shard_map/dot_general | solution.py:32
  474.9 0.0 copy-start.11
  475.0 0.0 copy-start.12
  475.0 0.0 copy-start.3
  475.0 0.0 reduce-scatter.4.cloned.1.call-update
  475.0 0.0 reduce-scatter.6.cloned.1.call-done
  475.1 0.7 copy-done.7
  475.8 0.0 copy-done.8
  475.8 0.0 copy-done.9
  475.8 1.5 multiply_subtract_fusion.2
  477.4 113.3 %reduce-scatter.8.cloned.1.call-done = f32[8,2048]{1,0:T(8,128)} async-done(((f32[256,2048]{1,0:T(8,128)}), f32[8,2048]{1,0:T(8,128)}) %reduce-scatter.8.cloned.1.call-update) | async-done | bytes 65552 | tf_op jit(solution)/shard_map/reduce_scatter | solution.py:134
  590.7 1.5 multiply_subtract_fusion.1
  592.2 192.9 %reduce-scatter.4.cloned.1.call-done = f32[64,2048]{1,0:T(8,128)} async-done(((f32[2048,2048]{1,0:T(8,128)}), f32[64,2048]{1,0:T(8,128)}) %reduce-scatter.4.cloned.1.call-update) | async-done | bytes 524304 | tf_op jit(solution)/shard_map/reduce_scatter | solution.py:126
  785.2 2.4 multiply_subtract_fusion
  (23 shorter events, 0.1 us)
Async XLA Ops:
  7.2 1.2 copy-start
  7.2 100.2 %all-reduce.3.cloned.1.call-start = ((), (), s32[]{:S(2)}) async-start(), calls=%async_computation.3 | async-start | bytes 2097152 | tf_op jit(solution)/shard_map/psum | solution.py:16
  8.4 6.1 copy-start.6
  14.5 255.0 %copy-start.1 = (f32[256,2048]{1,0:T(8,128)}, f32[256,2048]{1,0:T(8,128)S(1)}, u32[]{:S(2)}) copy-start(f32[256,2048]{1,0:T(8,128)S(1)} %get-tuple-element.65) | copy-start | bytes 6291460
  14.6 1.6 copy-start.13
  16.1 253.4 %all-reduce.5.cloned.1.call-start = ((), (), s32[]{:S(2)}) async-start(), calls=%async_computation.4 | async-start | bytes 4194304 | tf_op jit(solution)/shard_map/psum | solution.py:102
  145.7 3.2 copy-start.14
  148.8 326.2 %reduce-scatter.6.cloned.1.call-start = ((), (), s32[]{:S(2)}) async-start(), calls=%async_computation.6 | async-start | bytes 2162688 | tf_op jit(solution)/shard_map/reduce_scatter | solution.py:113
  152.0 438.6 %reduce-scatter.8.cloned.1.call-start = ((), (), s32[]{:S(2)}) async-start(), calls=%async_computation.7 | async-start | bytes 2162688 | tf_op jit(solution)/shard_map/reduce_scatter | solution.py:134
  269.5 2.2 copy-start.2
  273.8 32.1 %collective-permute-start = (bf16[256,2048]{1,0:T(8,128)(2,1)S(1)}, bf16[256,2048]{1,0:T(8,128)(2,1)S(1)}, u32[]{:S(2)}, u32[]{:S(2)}) collective-permute-start(bf16[256,2048]{1,0:T(8,128)(2,1)S(1)} %get-tuple-element.92), channel_id=1, source_target_pairs={{32,0},{64,32},{96,64},{128,96},{160,128},{192,160},{224,192},{33,... | collective-permute-start | bytes 3145736 | tf_op jit(solution)/shard_map/while/body/eval_jaxpr/ppermute | solution.py:22
  306.2 30.8 %collective-permute-start = (bf16[256,2048]{1,0:T(8,128)(2,1)S(1)}, bf16[256,2048]{1,0:T(8,128)(2,1)S(1)}, u32[]{:S(2)}, u32[]{:S(2)}) collective-permute-start(bf16[256,2048]{1,0:T(8,128)(2,1)S(1)} %get-tuple-element.92), channel_id=1, source_target_pairs={{32,0},{64,32},{96,64},{128,96},{160,128},{192,160},{224,192},{33,... | collective-permute-start | bytes 3145736 | tf_op jit(solution)/shard_map/while/body/eval_jaxpr/ppermute | solution.py:22
  337.2 30.7 %collective-permute-start = (bf16[256,2048]{1,0:T(8,128)(2,1)S(1)}, bf16[256,2048]{1,0:T(8,128)(2,1)S(1)}, u32[]{:S(2)}, u32[]{:S(2)}) collective-permute-start(bf16[256,2048]{1,0:T(8,128)(2,1)S(1)} %get-tuple-element.92), channel_id=1, source_target_pairs={{32,0},{64,32},{96,64},{128,96},{160,128},{192,160},{224,192},{33,... | collective-permute-start | bytes 3145736 | tf_op jit(solution)/shard_map/while/body/eval_jaxpr/ppermute | solution.py:22
  368.2 27.7 %collective-permute-start = (bf16[256,2048]{1,0:T(8,128)(2,1)S(1)}, bf16[256,2048]{1,0:T(8,128)(2,1)S(1)}, u32[]{:S(2)}, u32[]{:S(2)}) collective-permute-start(bf16[256,2048]{1,0:T(8,128)(2,1)S(1)} %get-tuple-element.92), channel_id=1, source_target_pairs={{32,0},{64,32},{96,64},{128,96},{160,128},{192,160},{224,192},{33,... | collective-permute-start | bytes 3145736 | tf_op jit(solution)/shard_map/while/body/eval_jaxpr/ppermute | solution.py:22
  396.3 23.2 %collective-permute-start = (bf16[256,2048]{1,0:T(8,128)(2,1)S(1)}, bf16[256,2048]{1,0:T(8,128)(2,1)S(1)}, u32[]{:S(2)}, u32[]{:S(2)}) collective-permute-start(bf16[256,2048]{1,0:T(8,128)(2,1)S(1)} %get-tuple-element.92), channel_id=1, source_target_pairs={{32,0},{64,32},{96,64},{128,96},{160,128},{192,160},{224,192},{33,... | collective-permute-start | bytes 3145736 | tf_op jit(solution)/shard_map/while/body/eval_jaxpr/ppermute | solution.py:22
  419.8 21.7 %collective-permute-start = (bf16[256,2048]{1,0:T(8,128)(2,1)S(1)}, bf16[256,2048]{1,0:T(8,128)(2,1)S(1)}, u32[]{:S(2)}, u32[]{:S(2)}) collective-permute-start(bf16[256,2048]{1,0:T(8,128)(2,1)S(1)} %get-tuple-element.92), channel_id=1, source_target_pairs={{32,0},{64,32},{96,64},{128,96},{160,128},{192,160},{224,192},{33,... | collective-permute-start | bytes 3145736 | tf_op jit(solution)/shard_map/while/body/eval_jaxpr/ppermute | solution.py:22
  441.8 22.9 %collective-permute-start = (bf16[256,2048]{1,0:T(8,128)(2,1)S(1)}, bf16[256,2048]{1,0:T(8,128)(2,1)S(1)}, u32[]{:S(2)}, u32[]{:S(2)}) collective-permute-start(bf16[256,2048]{1,0:T(8,128)(2,1)S(1)} %get-tuple-element.92), channel_id=1, source_target_pairs={{32,0},{64,32},{96,64},{128,96},{160,128},{192,160},{224,192},{33,... | collective-permute-start | bytes 3145736 | tf_op jit(solution)/shard_map/while/body/eval_jaxpr/ppermute | solution.py:22
  466.8 318.4 %reduce-scatter.4.cloned.1.call-start = ((), (), s32[]{:S(2)}) async-start(), calls=%async_computation.5 | async-start | bytes 17301504 | tf_op jit(solution)/shard_map/reduce_scatter | solution.py:126
  474.9 0.8 copy-start.7
  474.9 0.9 copy-start.8
  474.9 0.9 copy-start.9
  474.9 115.7 %copy-start.10 = (f32[8,2048]{1,0:T(8,128)S(1)}, f32[8,2048]{1,0:T(8,128)}, u32[]{:S(2)}) copy-start(f32[8,2048]{1,0:T(8,128)} %param.31) | copy-start | bytes 196612
  474.9 115.7 %copy-start.11 = (f32[8,2048]{1,0:T(8,128)S(1)}, f32[8,2048]{1,0:T(8,128)}, u32[]{:S(2)}) copy-start(f32[8,2048]{1,0:T(8,128)} %param.33) | copy-start | bytes 196612
  475.0 115.7 %copy-start.12 = (f32[8,2048]{1,0:T(8,128)S(1)}, f32[8,2048]{1,0:T(8,128)}, u32[]{:S(2)}) copy-start(f32[8,2048]{1,0:T(8,128)} %param.32) | copy-start | bytes 196612
  475.0 310.2 %copy-start.3 = (f32[1,64,2048]{2,1,0:T(8,128)S(1)}, f32[1,64,2048]{2,1,0:T(8,128)}, u32[]{:S(2)}) copy-start(f32[1,64,2048]{2,1,0:T(8,128)} %param.25) | copy-start | bytes 1572868
  475.0 310.2 %copy-start.4 = (f32[1,64,2048]{2,1,0:T(8,128)S(1)}, f32[1,64,2048]{2,1,0:T(8,128)}, u32[]{:S(2)}) copy-start(f32[1,64,2048]{2,1,0:T(8,128)} %param.27) | copy-start | bytes 1572868
  475.0 310.2 %copy-start.5 = (f32[1,64,2048]{2,1,0:T(8,128)S(1)}, f32[1,64,2048]{2,1,0:T(8,128)}, u32[]{:S(2)}) copy-start(f32[1,64,2048]{2,1,0:T(8,128)} %param.26) | copy-start | bytes 1572868
Sparse Core Ops, SparseCore 0:
  16.2 91.1 all-reduce.2
  149.0 120.5 all-reduce.4
  272.0 116.3 reduce-scatter.5
  466.9 123.7 reduce-scatter.7
  593.1 192.0 reduce-scatter.3
where the time goes:
time: 798 us; the launch traced here: 794 us
  waiting for transfers between devices  684 us (86%)
  blocking collectives  36.2 us (5%)
  matrix products  24.2 us (3%)
  starting transfers between devices  20.1 us (3%)
  between operations  13.9 us (2%)
  other arithmetic  13.2 us (2%)
    reduce_scatter x1, waiting for transfers between devices, per_device(): lax.psum_scatter(out_term, 'dp', scatter_dimension=0, tiled=True)  193 us
    ppermute x7, waiting for transfers between devices, shifted_2(): lax.ppermute(value, axis, [(source, source + steps) for source in range(l...  169 us
    psum x1, waiting for transfers between devices, per_device(): lax.psum(plain_times(logit_cotangent, head_weight), 'section')  117 us
    reduce_scatter x1, waiting for transfers between devices, per_device(): lax.psum_scatter(embed_term(lax.axis_size('dp') * embed_master.shape[0]),...  113 us
    psum x1, waiting for transfers between devices, broadcast(): return lax.psum(kept, axis)  91.2 us
    ppermute x7, starting transfers between devices, shifted_2(): lax.ppermute(value, axis, [(source, source + steps) for source in range(l...  19.9 us
    psum x1, blocking collectives, per_device(): row_total = lax.psum(jnp.sum(shifted, axis=1), 'section')  18.1 us
    pmax x1, blocking collectives, per_device(): row_top = lax.pmax(local_top, 'section')  18 us
  transfers between devices with their start and end apart: 12, of which 11 were waited for; matrix products, arithmetic and copies ran while one was open for 3% of the time, Pallas kernels for 0%

commit v1 on v0

v1 whole, which is shorter than its diff:
```python
import jax
import jax.numpy as jnp
from jax import lax
from jax.experimental import pallas as pl
from jax.experimental.pallas import tpu as pltpu
from jax.sharding import PartitionSpec as P

norm_eps = 1e-05
beta_first = 0.9
beta_second = 0.95
adam_eps = 1e-05
learning_rate = 0.0003
decay_rate = 0.1
MESH = pl.DeviceIdType.MESH
bf16, f32 = jnp.bfloat16, jnp.float32
SECTIONS, REPLICAS = 8, 32
TOKENS, WIDTH, VOCAB = 256, 2048, 2048
BLOCK = TOKENS // SECTIONS
SLICE = VOCAB // SECTIONS
OWNED = 64
NT = (((1,), (1,)), ((), ()))
TN = (((0,), (0,)), ((), ()))


def dot(a, b, dims):
    return lax.dot_general(a, b, dims, preferred_element_type=f32)


def y_peer(y, k):
    return (y, y + 1 - 2 * (y % 2), (y + 2) % 4, 3 - y)[k]


def flip(value, k):
    return 1 - value if k else value


def kernel(
    wide_hbm, mixed_hbm, head_hbm, weight_hbm, gain, targets, ids,
    out_grad, head_grad, embed_grad,
    mix, hd, wbuf, wide, final, hid, stats, hmine, smine, lg, lcb, hc, cotb,
    gcot, bcot, ghid, bhid, alog, idsb, psum, psend, rs, rs0, tile_e, tile_h, er, hr,
    loc, hs, hrv, fs, fr, ms, mr, ns, nr, ts, tr, ls, lr, gs, gr, cs, cr, is_, ir,
    vs, vr, ws, wr, rss, rsr, es, erv, zs, zr,
):
    section = lax.axis_index("section")
    replica = lax.axis_index("dp")
    y, xh = section // 2, section % 2
    z, xl, c = replica // 4, (replica // 2) % 2, replica % 2
    sigma = 1 - 2 * (z % 2)
    root = section == SECTIONS - 1

    def dev(y_, xh_, z_, xl_, c_):
        return (y_ * 2 + xh_, z_ * 4 + xl_ * 2 + c_)

    def section_peer(j, cross=False):
        ky, kx = j // 2, j % 2
        return dev(y_peer(y, ky), flip(xh, kx), z, flip(xl, kx) if cross else xl, c)

    def member(m):
        kz, kl, kc = m // 4, (m // 2) % 2, m % 2
        return (z + 4 * kz) % 8, flip(xl, kl), flip(c, kc)

    def remote(src, dst, send, recv, device):
        return pltpu.make_async_remote_copy(
            src_ref=src, dst_ref=dst, send_sem=send, recv_sem=recv,
            device_id=device, device_id_type=MESH,
        )

    load_mix = pltpu.make_async_copy(mixed_hbm, mix.at[0], loc.at[0])
    load_head = pltpu.make_async_copy(head_hbm, hd.at[section], loc.at[1])
    load_mix.start()
    load_head.start()
    load_wide = pltpu.make_async_copy(wide_hbm, wide, loc.at[2])

    def load_weight(n):
        return pltpu.make_async_copy(weight_hbm.at[pl.ds(n * 256, 256)], wbuf.at[n], loc.at[4 + n])

    @pl.when(root)
    def _():
        load_wide.start()
        for n in range(8):
            load_weight(n).start()

    barrier = pltpu.get_barrier_semaphore()
    for j in range(1, 8):
        pl.semaphore_signal(barrier, inc=1, device_id=section_peer(j), device_id_type=MESH)
        if j % 2:
            pl.semaphore_signal(barrier, inc=1, device_id=section_peer(j, True), device_id_type=MESH)

    def greet(k, carry):
        pl.semaphore_signal(
            barrier, inc=1, device_id=(section, (replica + k) % REPLICAS), device_id_type=MESH
        )
        return carry

    lax.fori_loop(1, REPLICAS, greet, 0)
    pl.semaphore_wait(barrier, 7 + 4 + REPLICAS - 1)

    half = pl.ds(pl.multiple_of(c * 128, 128), 128)
    load_head.wait()
    head_sends = []
    for j in (2, 6, 1, 4, 3, 7, 5):
        own = hd.at[section, half]
        copy = remote(own, own, hs.at[j], hrv.at[j], section_peer(j, True))
        copy.start()
        head_sends.append(copy)
    load_mix.wait()
    partner = dev(y, xh, z, xl, 1 - c)

    def mix_copy(src, dst, device):
        return remote(mix.at[src], mix.at[dst], ms.at[dst], mr.at[dst], device)

    mix_xl = mix_copy(0, 2, dev(y, xh, z, 1 - xl, c))
    mix_z = mix_copy(0, 4, dev(y, xh, (z + 4) % 8, xl, c))
    mix_diag = mix_copy(4, 6, dev(y, xh, z, 1 - xl, c))
    mix_core = [mix_copy(m, m + 1, partner) for m in (0, 2, 4, 6)]
    mix_z.start()
    mix_xl.start()
    mix_core[0].start()
    own_ids = pltpu.make_async_copy(ids, idsb.at[0], loc.at[3])
    own_ids.start()
    ids_sends = []
    for m in range(1, 8):
        copy = remote(ids, idsb.at[m], is_.at[m], ir.at[m], dev(y, xh, *member(m)))
        copy.start()
        ids_sends.append(copy)

    def hidden_send(j):
        ky, kx = j // 2, j % 2
        peer = section_peer(j)
        rows = pl.ds(pl.multiple_of(peer[0] * BLOCK, BLOCK), BLOCK)
        return (
            remote(hid.at[rows], hmine, ts.at[0, j], tr.at[0], peer),
            remote(stats.at[rows], smine, ts.at[1, j], tr.at[1], peer),
        )

    @pl.when(root)
    def _():
        load_wide.wait()
        for n in range(8):
            load_weight(n).wait()

        def columns(n, carry):
            cols = pl.ds(pl.multiple_of(n * 256, 256), 256)
            final[:, cols] = dot(mix[0], wbuf[n], NT) + wide[:, cols].astype(f32)
            return carry

        lax.fori_loop(0, 8, columns, 0)

        def norm(b, carry):
            rows = pl.ds(pl.multiple_of(b * BLOCK, BLOCK), BLOCK)
            values = final[rows, :]
            inverse = lax.rsqrt(jnp.mean(values * values, axis=-1, keepdims=True) + norm_eps)
            hid[rows, :] = (values * inverse * gain[...]).astype(bf16)
            stats[rows, :] = jnp.broadcast_to(inverse, (BLOCK, 128))
            return carry

        lax.fori_loop(0, SECTIONS, norm, 0)
        for j in (4, 5, 1, 3, 7, 2, 6):
            for copy in hidden_send(j):
                copy.start()
        hmine[...] = hid[(SECTIONS - 1) * BLOCK :, :]
        smine[...] = stats[(SECTIONS - 1) * BLOCK :, :]

    def sender_slice(j):
        ky, kx = j // 2, j % 2
        return y_peer(y, ky) * 2 + flip(xh, kx)

    forwards = []
    for j in (2, 6, 1, 4, 3, 7, 5):
        part = hd.at[sender_slice(j), half]
        remote(part, part, hs.at[j], hrv.at[j], section_peer(j, True)).wait_recv()
        copy = remote(part, part, fs.at[j], fr.at[j], partner)
        copy.start()
        forwards.append(copy)
    mix_xl.wait_recv()
    mix_core[1].start()

    @pl.when(jnp.logical_not(root))
    def _():
        for copy in hidden_send(1):
            copy.wait_recv()

    def four(n):
        return dev(y, xh, z, flip(xl, n // 2), flip(c, n % 2))

    hid_sends = []
    for n in range(4):
        peer_column = flip(xl, n // 2) * 2 + flip(c, n % 2)
        src = hmine.at[:, pl.ds(pl.multiple_of(peer_column * 512, 512), 512)]
        if n == 0:
            copy = pltpu.make_async_copy(src, ghid.at[0], nr.at[0])
        else:
            copy = remote(src, ghid.at[n], ns.at[n], nr.at[n], four(n))
        copy.start()
        hid_sends.append(copy)
    for copy in forwards:
        copy.wait_recv()

    def logits(n, carry):
        lg[:, pl.ds(pl.multiple_of(n * SLICE, SLICE), SLICE)] = dot(hmine[...], hd[n], NT)
        return carry

    lax.fori_loop(0, SECTIONS, logits, 0)
    values = lg[...]
    shifted = jnp.exp(values - jnp.max(values, axis=1, keepdims=True))
    predicted = shifted / jnp.sum(shifted, axis=1, keepdims=True)
    columns_ = lax.broadcasted_iota(jnp.int32, (BLOCK, VOCAB), 1)
    lcb[...] = jnp.where(targets[...] == columns_, predicted - 1.0, predicted).astype(bf16)

    mine = pl.ds(pl.multiple_of(section * BLOCK, BLOCK), BLOCK)
    log_sends = []
    for j in range(8):
        peer_section = sender_slice(j)
        src = lcb.at[:, pl.ds(pl.multiple_of(peer_section * SLICE, SLICE), SLICE)]
        dst = alog.at[0, mine]
        if j == 0:
            copy = pltpu.make_async_copy(src, dst, lr.at[0])
        else:
            copy = remote(src, dst, ls.at[j], lr.at[j], section_peer(j))
        copy.start()
        log_sends.append(copy)

    def back(n, carry):
        cols = pl.ds(pl.multiple_of(n * 256, 256), 256)
        total = jnp.zeros((BLOCK, 256), f32)
        for s in range(SECTIONS):
            total += jnp.dot(
                lcb[:, s * SLICE : (s + 1) * SLICE], hd[s, :, cols], preferred_element_type=f32
            )
        hc[:, cols] = total
        return carry

    lax.fori_loop(0, WIDTH // 256, back, 0)
    scaled = hc[...] * gain[...]
    unit = hmine[...].astype(f32) / gain[...]
    inverse = smine[:, :1]
    along = jnp.mean(scaled * unit, axis=-1, keepdims=True)
    cotb[...] = (inverse * (scaled - unit * along)).astype(bf16)

    def offset(c_, part):
        low = (0, 1)[part]
        high = (-1, 2)[part]
        return sigma * (low + (high - low) * c_)

    def column_block(z_, xl_, c_, part):
        return ((z_ + offset(c_, part) + 8) % 8) * 2 + xl_

    cot_sends = []
    for m in (4, 5, 6, 7, 2, 3, 1, 0):
        z_, xl_, c_ = member(m)
        for part in range(2):
            block = column_block(z_, xl_, c_, part)
            src = cotb.at[:, pl.ds(pl.multiple_of(block * 128, 128), 128)]
            dst = gcot.at[m, :, pl.ds(part * 128, 128)]
            if m == 0:
                copy = pltpu.make_async_copy(src, dst, gr.at[m, part])
            else:
                copy = remote(src, dst, gs.at[m, part], gr.at[m, part], dev(y, xh, z_, xl_, c_))
            copy.start()
            cot_sends.append((m, copy))

    mix_z.wait_recv()
    mix_diag.start()
    mix_core[2].start()

    for m, copy in cot_sends:
        if m == 0:
            copy.wait()
        else:
            copy.wait_recv()
    all_sends = []
    for j in (6, 7, 4, 5, 1, 2, 3, 0):
        dst = bcot.at[:, mine]
        if j == 0:
            copy = pltpu.make_async_copy(gcot, dst, cr.at[0])
        else:
            copy = remote(gcot, dst, cs.at[j], cr.at[j], section_peer(j))
        copy.start()
        all_sends.append((j, copy))

    for j, copy in enumerate(log_sends):
        if j == 0:
            copy.wait()
        else:
            copy.wait_recv()
    log_group = []
    for n in range(1, 4):
        copy = remote(alog.at[0], alog.at[n], vs.at[n], vr.at[n], four(n))
        copy.start()
        log_group.append(copy)
    for n, copy in enumerate(hid_sends):
        if n == 0:
            copy.wait()
        else:
            copy.wait_recv()
    hid_all = []
    for j in (6, 7, 4, 5, 1, 2, 3, 0):
        dst = bhid.at[:, mine]
        if j == 0:
            copy = pltpu.make_async_copy(ghid, dst, wr.at[0])
        else:
            copy = remote(ghid, dst, ws.at[j], wr.at[j], section_peer(j))
        copy.start()
        hid_all.append((j, copy))

    mix_diag.wait_recv()
    mix_core[3].start()
    for copy in mix_core:
        copy.wait_recv()
    own_ids.wait()
    for copy in ids_sends:
        copy.wait_recv()
    for j, copy in all_sends:
        if j == 0:
            copy.wait()
        else:
            copy.wait_recv()

    def product(n, carry):
        cols = pl.ds(pl.multiple_of(n * 256, 256), 256)
        total = jnp.zeros((256, 256), f32)
        for m in range(8):
            total += dot(bcot[m], mix[m, :, cols], TN)
        psum[:, cols] = total
        psend[:, cols] = total.astype(bf16)
        return carry

    lax.fori_loop(0, WIDTH // 256, product, 0)

    def owner(part, c_):
        return dev(y, xh, (z + offset(c, part) + 8) % 8, xl, c_)

    def partial_rows(part, c_):
        return pl.ds((part * 2 + c_) * OWNED, OWNED)

    def far_copy(part, slot, c_):
        return remote(
            psend.at[partial_rows(part, c_)], rs.at[slot], rss.at[part, c_], rsr.at[slot], owner(part, c_)
        )

    near_copy = remote(psum.at[partial_rows(0, 1)], rs0, rss.at[0, 1], rsr.at[3], partner)

    @pl.when(c == 0)
    def _():
        far_copy(1, 1, 0).start()
        far_copy(1, 1, 1).start()
        near_copy.start()
        rs0[...] = psum[:OWNED, :]

    @pl.when(c == 1)
    def _():
        far_copy(1, 2, 0).start()
        far_copy(1, 2, 1).start()
        far_copy(0, 0, 0).start()
        far_copy(0, 0, 1).start()

    rows_ = section * SLICE + lax.broadcasted_iota(jnp.int32, (SLICE, TOKENS), 0)
    embed = jnp.zeros((SLICE, 256), f32)
    for m in range(8):
        marks = (idsb[m, :1, :] == rows_).astype(f32).astype(bf16)
        embed += jnp.dot(marks, bcot[m], preferred_element_type=f32)
    tile_e[...] = embed.reshape(REPLICAS, 8, 256)

    blocks = [column_block(z, xl, c, part) for part in range(2)]

    def embed_copy(target, part):
        cols = pl.ds(pl.multiple_of(blocks[part] * 128, 128), 128)
        return tile_e.at[target, :, pl.ds(part * 128, 128)], er.at[z % 4, :, cols]

    def send_embed(k, carry):
        target = (replica + k) % REPLICAS
        for part in range(2):
            src, dst = embed_copy(target, part)
            remote(src, dst, es.at[0], erv.at[0], (section, target)).start()
        return carry

    lax.fori_loop(1, REPLICAS, send_embed, 0)
    for part in range(2):
        src, dst = embed_copy(replica, part)
        pltpu.make_async_copy(src, dst, erv.at[0]).start()

    for copy in log_group:
        copy.wait_recv()
    for j, copy in hid_all:
        if j == 0:
            copy.wait()
        else:
            copy.wait_recv()

    head = jnp.zeros((SLICE, 512), f32)
    for n in range(4):
        head += dot(alog[n], bhid[n], TN)
    tile_h[...] = head.reshape(REPLICAS, 8, 512)
    head_cols = pl.ds(pl.multiple_of((xl * 2 + c) * 512, 512), 512)

    def send_head(k, carry):
        target = (replica + k) % REPLICAS
        remote(tile_h.at[target], hr.at[z, :, head_cols], zs.at[0], zr.at[0], (section, target)).start()
        return carry

    lax.fori_loop(1, REPLICAS, send_head, 0)
    pltpu.make_async_copy(tile_h.at[replica], hr.at[z, :, head_cols], zr.at[0]).start()

    @pl.when(c == 1)
    def _():
        near_copy.wait_recv()

    for slot in range(3):
        far_copy(1, slot, 0).wait_recv()
    out_grad[...] = (
        rs0[...] + rs[0].astype(f32) + rs[1].astype(f32) + rs[2].astype(f32)
    )
    pltpu.make_async_copy(er, er, erv.at[0]).wait()
    embed_grad[...] = er[0] + er[1] + er[2] + er[3]
    pltpu.make_async_copy(hr, hr, zr.at[0]).wait()
    total = hr[0]
    for k in range(1, 8):
        total += hr[k]
    head_grad[...] = total

    for copy in head_sends + forwards + mix_core + ids_sends + log_group + [mix_xl, mix_z, mix_diag]:
        copy.wait_send()
    for copies in (hid_sends, log_sends):
        for copy in copies[1:]:
            copy.wait_send()
    for copies in (cot_sends, all_sends, hid_all):
        for index, copy in copies:
            if index:
                copy.wait_send()

    @pl.when(root)
    def _():
        for j in range(1, 8):
            for copy in hidden_send(j):
                copy.wait_send()

    @pl.when(c == 0)
    def _():
        far_copy(1, 1, 0).wait_send()
        far_copy(1, 1, 1).wait_send()
        near_copy.wait_send()

    @pl.when(c == 1)
    def _():
        for part in range(2):
            for c_ in range(2):
                far_copy(part, 0, c_).wait_send()

    sent = tile_e.at[pl.ds(0, REPLICAS - 1)]
    pltpu.make_async_copy(sent, sent, es.at[0]).wait()
    sent = tile_h.at[pl.ds(0, REPLICAS - 1)]
    pltpu.make_async_copy(sent, sent, zs.at[0]).wait()


def gradients(wide, mixed, head, weight, gain, targets, ids):
    dma = pltpu.SemaphoreType.DMA
    vm = pltpu.VMEM
    any_ = pl.BlockSpec(memory_space=pl.ANY)
    vmem = pl.BlockSpec(memory_space=pltpu.VMEM)
    return pl.pallas_call(
        kernel,
        out_shape=(
            jax.ShapeDtypeStruct((OWNED, WIDTH), f32),
            jax.ShapeDtypeStruct((8, WIDTH), f32),
            jax.ShapeDtypeStruct((8, WIDTH), f32),
        ),
        in_specs=[any_] * 4 + [vmem] * 3,
        out_specs=(vmem,) * 3,
        scratch_shapes=[
            vm((8, TOKENS, WIDTH), bf16),
            vm((SECTIONS, SLICE, WIDTH), bf16),
            vm((8, 256, WIDTH), bf16),
            vm((TOKENS, WIDTH), bf16),
            vm((TOKENS, WIDTH), f32),
            vm((TOKENS, WIDTH), bf16),
            vm((TOKENS, 128), f32),
            vm((BLOCK, WIDTH), bf16),
            vm((BLOCK, 128), f32),
            vm((BLOCK, VOCAB), f32),
            vm((BLOCK, VOCAB), bf16),
            vm((BLOCK, WIDTH), f32),
            vm((BLOCK, WIDTH), bf16),
            vm((8, BLOCK, 256), bf16),
            vm((8, TOKENS, 256), bf16),
            vm((4, BLOCK, 512), bf16),
            vm((4, TOKENS, 512), bf16),
            vm((4, TOKENS, SLICE), bf16),
            vm((8, 8, TOKENS), jnp.int32),
            vm((256, WIDTH), f32),
            vm((256, WIDTH), bf16),
            vm((3, OWNED, WIDTH), bf16),
            vm((OWNED, WIDTH), f32),
            vm((REPLICAS, 8, 256), f32),
            vm((REPLICAS, 8, 512), f32),
            vm((4, 8, WIDTH), f32),
            vm((8, 8, WIDTH), f32),
            dma((12,)),
            dma((8,)), dma((8,)),
            dma((8,)), dma((8,)),
            dma((8,)), dma((8,)),
            dma((4,)), dma((4,)),
            dma((2, 8)), dma((2,)),
            dma((8,)), dma((8,)),
            dma((8, 2)), dma((8, 2)),
            dma((8,)), dma((8,)),
            dma((8,)), dma((8,)),
            dma((4,)), dma((4,)),
            dma((8,)), dma((8,)),
            dma((2, 2)), dma((4,)),
            dma((1,)), dma((1,)),
            dma((1,)), dma((1,)),
        ],
        compiler_params=pltpu.CompilerParams(
            collective_id=0, has_side_effects=True, vmem_limit_bytes=60 * 2**20
        ),
    )(wide, mixed, head, weight, gain, targets, ids)


def adam_update(master, first, second, gradient):
    first_next = beta_first * first + (1.0 - beta_first) * gradient
    second_next = beta_second * second + (1.0 - beta_second) * gradient * gradient
    master_next = master - learning_rate * (
        first_next / (jnp.sqrt(second_next) + adam_eps) + decay_rate * master
    )
    return (master_next, first_next, second_next)


def per_device(
    block_inputs, mixed_inputs, token_ids, target_ids, final_gain, out_weight, head_weight,
    out_master, out_first, out_second, head_master, head_first, head_second,
    embed_master, embed_first, embed_second,
):
    section = lax.axis_index("section")
    targets = lax.dynamic_slice_in_dim(target_ids.reshape(TOKENS, 1), section * BLOCK, BLOCK, 0)
    ids = jnp.broadcast_to(token_ids.reshape(1, TOKENS), (8, TOKENS))
    out_gradient, head_gradient, embed_gradient = gradients(
        block_inputs.reshape(TOKENS, WIDTH),
        mixed_inputs.reshape(TOKENS, WIDTH),
        head_weight,
        out_weight.reshape(WIDTH, WIDTH),
        final_gain.reshape(1, WIDTH),
        targets,
        ids,
    )
    return (
        *adam_update(out_master, out_first, out_second, out_gradient.reshape(out_master.shape)),
        *adam_update(head_master, head_first, head_second, head_gradient),
        *adam_update(embed_master, embed_first, embed_second, embed_gradient),
    )


def solution(mesh):
    tokens = P("section", None, "dp", None)
    rows = P("section", "dp", None)
    vocabulary = P(("section", "dp"), None)
    in_specs = (
        tokens, tokens, P(None, "dp"), P(None, "dp"), P(), P("section", None, None), P("section", None),
        rows, rows, rows, *(vocabulary,) * 6,
    )
    out_specs = (rows, rows, rows, *(vocabulary,) * 6)
    return jax.shard_map(
        per_device, mesh=mesh, in_specs=in_specs, out_specs=out_specs, check_vma=False
    )
```

time: 798 us -> 171 us (0.21)
  waiting for transfers between devices: 684 us -> 0 us
  Pallas kernels: 0 us -> 161 us
  blocking collectives: 36.2 us -> 0 us
  matrix products: 24.2 us -> 0 us
  starting transfers between devices: 20.1 us -> 0 us
  between operations: 13.9 us -> 0.79 us
  other arithmetic: 13.2 us -> 4.04 us
    reduce_scatter x3 -> x0, waiting for transfers between devices: 306 us -> none  [the longest x1 193 us: per_device(): lax.psum_scatter(out_term, 'dp', scatter_dimension=0, tiled=True)]
    psum x2 -> x0, waiting for transfers between devices: 209 us -> none  [the longest x1 117 us: per_device(): lax.psum(plain_times(logit_cotangent, head_weight), 'section')]
    ppermute x7 -> x0, waiting for transfers between devices: 169 us -> none  [shifted_2(): lax.ppermute(value, axis, [(source, source + steps) for source in range(l...]
    pallas_call x0 -> x1, Pallas kernels: none -> 161 us  [gradients(): pl.pallas_call(kernel, out_shape=(jax.ShapeDtypeStruct((OWNED, WIDTH), f3...]
    dot_general x6 -> x0, matrix products: 24.2 us -> none  [the longest x3 12.9 us: transposed_times(): lax.dot_general(former, latter, (((0,), (0,)), ((), ())), preferred_eleme...]
    ppermute x7 -> x0, starting transfers between devices: 19.9 us -> none  [shifted_2(): lax.ppermute(value, axis, [(source, source + steps) for source in range(l...]
    psum x1 -> x0, blocking collectives: 18.1 us -> none  [per_device(): row_total = lax.psum(jnp.sum(shifted, axis=1), 'section')]
    pmax x1 -> x0, blocking collectives: 18 us -> none  [per_device(): row_top = lax.pmax(local_top, 'section')]
  transfers between devices with their start and end apart: 12 -> 0, of which waited for: 11 -> 0; matrix products, arithmetic and copies ran while one was open for 3% -> 0% of each run, Pallas kernels for 0% -> 0%
where the time goes in v1:
time: 171 us; the launch traced here: 169 us
  Pallas kernels  161 us (94%)
  other arithmetic  4.04 us (2%)
  local copies, waits for them, and re-layouts  2.96 us (2%)
    pallas_call x1, Pallas kernels, gradients(): pl.pallas_call(kernel, out_shape=(jax.ShapeDtypeStruct((OWNED, WIDTH), f3...  161 us
    sub x2, other arithmetic, adam_update(): master - learning_rate * (first_next / (jnp.sqrt(second_next) + adam_eps)...  4.04 us

profile of v1, /device:TPU:7, one launch (start us, length us, event | category | flops | bytes accessed | tf_op | source)
XLA Modules:
  0.0 169.3 jit_solution(14280022529810261678)
XLA Ops:
  0.6 0.0 copy-start
  0.7 0.0 copy-start.1
  0.7 0.0 copy-start.2
  0.7 0.0 copy-start.3
  0.7 0.0 copy-start.4
  0.7 0.0 copy-start.5
  0.7 0.0 copy-start.6
  0.7 0.0 copy-start.7
  0.7 0.0 copy-start.8
  0.7 0.9 reshape.44
  1.7 0.6 constant_dynamic-slice_fusion.targets
  2.3 0.8 broadcast_in_dim.7
  3.1 0.6 broadcast_in_dim.8.ids
  3.7 161.5 %shard_map.223 = (f32[64,2048]{1,0:T(8,128)}, f32[8,2048]{1,0:T(8,128)}, f32[8,2048]{1,0:T(8,128)}) custom-call(bf16[256,2048]{1,0:T(8,128)(2,1)} %bitcast.13, bf16[256,2048]{1,0:T(8,128)(2,1)} %bitcast.14, bf16[256,2048]{1,0:T(8,128)(2,1)} %head_hbm.1, bf16[2048,2048]{1,0:T(8,128)(2,1)} %bitcast.12, f32[1,2048]{1,0:T(1,128)} %bitcast.15, ...), custom_call_target="tpu_custom_call" | custom-call | tf_op jit(solution)/shard_map/pallas_call | solution.py:461
  165.2 0.0 copy-done
  165.2 0.0 copy-done.1
  165.2 0.0 copy-done.2
  165.2 2.4 %multiply_subtract_fusion = (f32[1,64,2048]{2,1,0:T(8,128)}, f32[1,64,2048]{2,1,0:T(8,128)}, f32[1,64,2048]{2,1,0:T(8,128)}) fusion(f32[1,64,2048]{2,1,0:T(8,128)S(1)} %copy-done, f32[64,2048]{1,0:T(8,128)} %get-tuple-element.12, f32[1,64,2048]{2,1,0:T(8,128)S(1)} %copy-done.1, f32[1,64,2048]{2,1,0:T(8,128)S(1)} %copy-done.2), kind=kLoop, calls=%fused_computation.4 | loop fusion | flops 1703936 | bytes 3670016 | tf_op jit(solution)/shard_map/sub | solution.py:523
  167.6 0.0 copy-done.3
  167.6 0.0 copy-done.4
  167.6 0.0 copy-done.5
  167.6 0.0 copy-done.6
  167.6 0.0 copy-done.7
  167.6 0.0 copy-done.8
  167.6 1.7 multiply_subtract_fusion.1
Async XLA Ops:
  0.6 164.5 %copy-start = (f32[1,64,2048]{2,1,0:T(8,128)S(1)}, f32[1,64,2048]{2,1,0:T(8,128)}, u32[]{:S(2)}) copy-start(f32[1,64,2048]{2,1,0:T(8,128)} %param.23) | copy-start | bytes 1572868
  0.7 164.5 %copy-start.1 = (f32[1,64,2048]{2,1,0:T(8,128)S(1)}, f32[1,64,2048]{2,1,0:T(8,128)}, u32[]{:S(2)}) copy-start(f32[1,64,2048]{2,1,0:T(8,128)} %param.25) | copy-start | bytes 1572868
  0.7 164.5 %copy-start.2 = (f32[1,64,2048]{2,1,0:T(8,128)S(1)}, f32[1,64,2048]{2,1,0:T(8,128)}, u32[]{:S(2)}) copy-start(f32[1,64,2048]{2,1,0:T(8,128)} %param.24) | copy-start | bytes 1572868
  0.7 166.9 %copy-start.3 = (f32[8,2048]{1,0:T(8,128)S(1)}, f32[8,2048]{1,0:T(8,128)}, u32[]{:S(2)}) copy-start(f32[8,2048]{1,0:T(8,128)} %param.29) | copy-start | bytes 196612
  0.7 166.9 %copy-start.4 = (f32[8,2048]{1,0:T(8,128)S(1)}, f32[8,2048]{1,0:T(8,128)}, u32[]{:S(2)}) copy-start(f32[8,2048]{1,0:T(8,128)} %param.31) | copy-start | bytes 196612
  0.7 166.9 %copy-start.5 = (f32[8,2048]{1,0:T(8,128)S(1)}, f32[8,2048]{1,0:T(8,128)}, u32[]{:S(2)}) copy-start(f32[8,2048]{1,0:T(8,128)} %param.30) | copy-start | bytes 196612
  0.7 166.9 %copy-start.6 = (f32[8,2048]{1,0:T(8,128)S(1)}, f32[8,2048]{1,0:T(8,128)}, u32[]{:S(2)}) copy-start(f32[8,2048]{1,0:T(8,128)} %param.26) | copy-start | bytes 196612
  0.7 166.9 %copy-start.7 = (f32[8,2048]{1,0:T(8,128)S(1)}, f32[8,2048]{1,0:T(8,128)}, u32[]{:S(2)}) copy-start(f32[8,2048]{1,0:T(8,128)} %param.28) | copy-start | bytes 196612
  0.7 166.9 %copy-start.8 = (f32[8,2048]{1,0:T(8,128)S(1)}, f32[8,2048]{1,0:T(8,128)}, u32[]{:S(2)}) copy-start(f32[8,2048]{1,0:T(8,128)} %param.27) | copy-start | bytes 196612

commit v2 on v1

--- a/solution.py
+++ b/solution.py
@@ -35,12 +35,12 @@
 
 
 def kernel(
-    wide_hbm, mixed_hbm, head_hbm, weight_hbm, gain, targets, ids,
+    wide_hbm, mixed_hbm, head_hbm, weight_hbm, gain_in, target_ids, token_ids,
     out_grad, head_grad, embed_grad,
     mix, hd, wbuf, wide, final, hid, stats, hmine, smine, lg, lcb, hc, cotb,
-    gcot, bcot, ghid, bhid, alog, idsb, psum, psend, rs, rs0, tile_e, tile_h, er, hr,
+    gcot, bcot, ghid, bhid, alog, idsb, gain, psum, psend, rs, rs0, tile_e, tile_h, er, hr,
     loc, hs, hrv, fs, fr, ms, mr, ns, nr, ts, tr, ls, lr, gs, gr, cs, cr, is_, ir,
-    vs, vr, ws, wr, rss, rsr, es, erv, zs, zr,
+    vs, vr, ws, wr, rss, rsr, es, erv, zs, zr, fms, fmr,
 ):
     section = lax.axis_index("section")
     replica = lax.axis_index("dp")
@@ -97,13 +97,20 @@
     pl.semaphore_wait(barrier, 7 + 4 + REPLICAS - 1)
 
     half = pl.ds(pl.multiple_of(c * 128, 128), 128)
+    def sender_slice(j):
+        return y_peer(y, j // 2) * 2 + flip(xh, j % 2)
+
+    head_sends = {}
+
+    def head_send(slot, source, peer):
+        part = hd.at[sender_slice(source), half]
+        copy = remote(part, part, hs.at[slot], hrv.at[slot], section_peer(peer, True))
+        copy.start()
+        head_sends[slot] = copy
+
     load_head.wait()
-    head_sends = []
-    for j in (2, 6, 1, 4, 3, 7, 5):
-        own = hd.at[section, half]
-        copy = remote(own, own, hs.at[j], hrv.at[j], section_peer(j, True))
-        copy.start()
-        head_sends.append(copy)
+    for j in (1, 2, 6):
+        head_send(j, 0, j)
     load_mix.wait()
     partner = dev(y, xh, z, xl, 1 - c)
 
@@ -111,17 +118,29 @@
         return remote(mix.at[src], mix.at[dst], ms.at[dst], mr.at[dst], device)
 
     mix_xl = mix_copy(0, 2, dev(y, xh, z, 1 - xl, c))
-    mix_z = mix_copy(0, 4, dev(y, xh, (z + 4) % 8, xl, c))
-    mix_diag = mix_copy(4, 6, dev(y, xh, z, 1 - xl, c))
-    mix_core = [mix_copy(m, m + 1, partner) for m in (0, 2, 4, 6)]
-    mix_z.start()
-    mix_xl.start()
+    mix_core = [mix_copy(m, m + 1, partner) for m in (0, 2)]
+
+    def far_mix(src, dst, device):
+        rows = [pl.ds(k * 64, 64) for k in range(4)]
+        return [
+            remote(mix.at[src, r], mix.at[dst, r], fms.at[dst - 4, k], fmr.at[dst - 4, k], device)
+            for k, r in enumerate(rows)
+        ]
+
+    mix_z = far_mix(0, 4, dev(y, xh, (z + 4) % 8, xl, c))
+    mix_diag = far_mix(4, 6, dev(y, xh, z, 1 - xl, c))
+    core_z = far_mix(4, 5, partner)
+    core_diag = far_mix(6, 7, partner)
+    for copy in mix_z:
+        copy.start()
     mix_core[0].start()
-    own_ids = pltpu.make_async_copy(ids, idsb.at[0], loc.at[3])
-    own_ids.start()
+    idsb[0] = jnp.broadcast_to(
+        jnp.concatenate([token_ids[b : b + 1, :] for b in range(4)], axis=1), (8, TOKENS)
+    )
+    gain[...] = gain_in[...].reshape(1, WIDTH)
     ids_sends = []
     for m in range(1, 8):
-        copy = remote(ids, idsb.at[m], is_.at[m], ir.at[m], dev(y, xh, *member(m)))
+        copy = remote(idsb.at[0], idsb.at[m], is_.at[m], ir.at[m], dev(y, xh, *member(m)))
         copy.start()
         ids_sends.append(copy)
 
@@ -162,51 +181,74 @@
         hmine[...] = hid[(SECTIONS - 1) * BLOCK :, :]
         smine[...] = stats[(SECTIONS - 1) * BLOCK :, :]
 
-    def sender_slice(j):
-        ky, kx = j // 2, j % 2
-        return y_peer(y, ky) * 2 + flip(xh, kx)
-
-    forwards = []
-    for j in (2, 6, 1, 4, 3, 7, 5):
+    head_send(4, 0, 4)
+    mix_xl.start()
+
+    forwards = {}
+
+    def pass_on(j):
         part = hd.at[sender_slice(j), half]
         remote(part, part, hs.at[j], hrv.at[j], section_peer(j, True)).wait_recv()
         copy = remote(part, part, fs.at[j], fr.at[j], partner)
         copy.start()
-        forwards.append(copy)
-    mix_xl.wait_recv()
-    mix_core[1].start()
+        forwards[j] = copy
+
+    def pass_far(k):
+        mix_z[k].wait_recv()
+        mix_diag[k].start()
+        core_z[k].start()
+
+    pass_on(1)
+    head_send(3, 1, 2)
+    head_send(7, 1, 6)
+    pass_on(2)
+    pass_on(6)
+    pass_far(0)
+    pass_on(4)
+    head_send(5, 4, 1)
+    pass_far(1)
 
     @pl.when(jnp.logical_not(root))
     def _():
         for copy in hidden_send(1):
             copy.wait_recv()
 
-    def four(n):
-        return dev(y, xh, z, flip(xl, n // 2), flip(c, n % 2))
-
     hid_sends = []
-    for n in range(4):
-        peer_column = flip(xl, n // 2) * 2 + flip(c, n % 2)
-        src = hmine.at[:, pl.ds(pl.multiple_of(peer_column * 512, 512), 512)]
-        if n == 0:
+    for m in range(8):
+        z_, xl_, c_ = member(m)
+        block = (z_ // 4) * 4 + xl_ * 2 + c_
+        src = hmine.at[:, pl.ds(pl.multiple_of(block * 256, 256), 256)]
+        if m == 0:
             copy = pltpu.make_async_copy(src, ghid.at[0], nr.at[0])
         else:
-            copy = remote(src, ghid.at[n], ns.at[n], nr.at[n], four(n))
+            copy = remote(src, ghid.at[m], ns.at[m], nr.at[m], dev(y, xh, z_, xl_, c_))
         copy.start()
         hid_sends.append(copy)
-    for copy in forwards:
-        copy.wait_recv()
-
-    def logits(n, carry):
+
+    def logits(j):
+        n = sender_slice(j)
         lg[:, pl.ds(pl.multiple_of(n * SLICE, SLICE), SLICE)] = dot(hmine[...], hd[n], NT)
-        return carry
-
-    lax.fori_loop(0, SECTIONS, logits, 0)
+
+    logits(0)
+    for j in (1, 2, 6, 4):
+        forwards[j].wait_recv()
+        logits(j)
+    for j in (3, 7, 5):
+        pass_on(j)
+    for j in (3, 7, 5):
+        forwards[j].wait_recv()
+        logits(j)
     values = lg[...]
     shifted = jnp.exp(values - jnp.max(values, axis=1, keepdims=True))
     predicted = shifted / jnp.sum(shifted, axis=1, keepdims=True)
     columns_ = lax.broadcasted_iota(jnp.int32, (BLOCK, VOCAB), 1)
-    lcb[...] = jnp.where(targets[...] == columns_, predicted - 1.0, predicted).astype(bf16)
+    batch_row = target_ids[pl.ds(section // 2, 1), :].astype(f32)
+    lanes = lax.broadcasted_iota(jnp.int32, (BLOCK, 64), 1)
+    places = lax.broadcasted_iota(jnp.int32, (BLOCK, 64), 0) + (section % 2) * BLOCK
+    targets = jnp.sum(
+        jnp.where(lanes == places, jnp.broadcast_to(batch_row, (BLOCK, 64)), 0.0), axis=1, keepdims=True
+    )
+    lcb[...] = jnp.where(targets == columns_.astype(f32), predicted - 1.0, predicted).astype(bf16)
 
     mine = pl.ds(pl.multiple_of(section * BLOCK, BLOCK), BLOCK)
     log_sends = []
@@ -220,6 +262,8 @@
             copy = remote(src, dst, ls.at[j], lr.at[j], section_peer(j))
         copy.start()
         log_sends.append(copy)
+
+    pass_far(2)
 
     def back(n, carry):
         cols = pl.ds(pl.multiple_of(n * 256, 256), 256)
@@ -260,9 +304,28 @@
             copy.start()
             cot_sends.append((m, copy))
 
-    mix_z.wait_recv()
-    mix_diag.start()
-    mix_core[2].start()
+    pass_far(3)
+    mix_xl.wait_recv()
+    mix_core[1].start()
+
+    for n, copy in enumerate(hid_sends):
+        if n == 0:
+            copy.wait()
+        else:
+            copy.wait_recv()
+    hid_all = []
+
+    def gather_hidden(j):
+        dst = bhid.at[:, mine]
+        if j == 0:
+            copy = pltpu.make_async_copy(ghid, dst, wr.at[0])
+        else:
+            copy = remote(ghid, dst, ws.at[j], wr.at[j], section_peer(j))
+        copy.start()
+        hid_all.append((j, copy))
+
+    for j in (2, 6, 4, 0):
+        gather_hidden(j)
 
     for m, copy in cot_sends:
         if m == 0:
@@ -284,31 +347,25 @@
             copy.wait()
         else:
             copy.wait_recv()
-    log_group = []
-    for n in range(1, 4):
-        copy = remote(alog.at[0], alog.at[n], vs.at[n], vr.at[n], four(n))
-        copy.start()
-        log_group.append(copy)
-    for n, copy in enumerate(hid_sends):
-        if n == 0:
-            copy.wait()
-        else:
-            copy.wait_recv()
-    hid_all = []
-    for j in (6, 7, 4, 5, 1, 2, 3, 0):
-        dst = bhid.at[:, mine]
-        if j == 0:
-            copy = pltpu.make_async_copy(ghid, dst, wr.at[0])
-        else:
-            copy = remote(ghid, dst, ws.at[j], wr.at[j], section_peer(j))
-        copy.start()
-        hid_all.append((j, copy))
-
-    mix_diag.wait_recv()
-    mix_core[3].start()
-    for copy in mix_core:
+    def log_copy(src, dst, device):
+        return remote(alog.at[src], alog.at[dst], vs.at[dst], vr.at[dst], device)
+
+    log_far = [log_copy(0, m, dev(y, xh, *member(m))) for m in (4, 6, 2)]
+    log_core = [log_copy(m, m + 1, partner) for m in (0, 2, 4, 6)]
+    for copy in log_far + log_core[:1]:
+        copy.start()
+    for j in (3, 7, 5, 1):
+        gather_hidden(j)
+
+    for k in range(4):
+        mix_diag[k].wait_recv()
+        core_diag[k].start()
+    for copy in mix_core + core_z + core_diag:
         copy.wait_recv()
-    own_ids.wait()
+    for copy in log_far:
+        copy.wait_recv()
+    for copy in log_core[1:]:
+        copy.start()
     for copy in ids_sends:
         copy.wait_recv()
     for j, copy in all_sends:
@@ -316,6 +373,31 @@
             copy.wait()
         else:
             copy.wait_recv()
+
+    rows_ = section * SLICE + lax.broadcasted_iota(jnp.int32, (SLICE, TOKENS), 0)
+    embed = jnp.zeros((SLICE, 256), f32)
+    for m in range(8):
+        marks = (idsb[m, :1, :] == rows_).astype(f32).astype(bf16)
+        embed += jnp.dot(marks, bcot[m], preferred_element_type=f32)
+    tile_e[...] = embed.reshape(REPLICAS, 8, 256)
+
+    blocks = [column_block(z, xl, c, part) for part in range(2)]
+
+    def embed_copy(target, part):
+        cols = pl.ds(pl.multiple_of(blocks[part] * 128, 128), 128)
+        return tile_e.at[target, :, pl.ds(part * 128, 128)], er.at[z % 4, :, cols]
+
+    def send_embed(k, carry):
+        target = (replica + k) % REPLICAS
+        for part in range(2):
+            src, dst = embed_copy(target, part)
+            remote(src, dst, es.at[0], erv.at[0], (section, target)).start()
+        return carry
+
+    lax.fori_loop(1, REPLICAS, send_embed, 0)
+    for part in range(2):
+        src, dst = embed_copy(replica, part)
+        pltpu.make_async_copy(src, dst, erv.at[0]).start()
 
     def product(n, carry):
         cols = pl.ds(pl.multiple_of(n * 256, 256), 256)
@@ -326,61 +408,46 @@
         psend[:, cols] = total.astype(bf16)
         return carry
 
-    lax.fori_loop(0, WIDTH // 256, product, 0)
-
     def owner(part, c_):
         return dev(y, xh, (z + offset(c, part) + 8) % 8, xl, c_)
 
     def partial_rows(part, c_):
         return pl.ds((part * 2 + c_) * OWNED, OWNED)
 
-    def far_copy(part, slot, c_):
+    def far_copy(part, slot, c_, h):
+        cols = pl.ds(h * (WIDTH // 2), WIDTH // 2)
         return remote(
-            psend.at[partial_rows(part, c_)], rs.at[slot], rss.at[part, c_], rsr.at[slot], owner(part, c_)
+            psend.at[partial_rows(part, c_), cols], rs.at[slot, :, cols],
+            rss.at[h, part, c_], rsr.at[h, slot], owner(part, c_),
         )
 
-    near_copy = remote(psum.at[partial_rows(0, 1)], rs0, rss.at[0, 1], rsr.at[3], partner)
+    def near_copy(h):
+        cols = pl.ds(h * (WIDTH // 2), WIDTH // 2)
+        return remote(
+            psum.at[partial_rows(0, 1), cols], rs0.at[:, cols], rss.at[h, 0, 1], rsr.at[h, 3], partner
+        )
+
+    for h in range(2):
+        lax.fori_loop(h * 4, h * 4 + 4, product, 0)
+
+        @pl.when(c == 0)
+        def _(h=h):
+            far_copy(1, 1, 0, h).start()
+            far_copy(1, 1, 1, h).start()
+            near_copy(h).start()
+
+        @pl.when(c == 1)
+        def _(h=h):
+            far_copy(1, 2, 0, h).start()
+            far_copy(1, 2, 1, h).start()
+            far_copy(0, 0, 0, h).start()
+            far_copy(0, 0, 1, h).start()
 
     @pl.when(c == 0)
     def _():
-        far_copy(1, 1, 0).start()
-        far_copy(1, 1, 1).start()
-        near_copy.start()
         rs0[...] = psum[:OWNED, :]
 
-    @pl.when(c == 1)
-    def _():
-        far_copy(1, 2, 0).start()
-        far_copy(1, 2, 1).start()
-        far_copy(0, 0, 0).start()
-        far_copy(0, 0, 1).start()
-
-    rows_ = section * SLICE + lax.broadcasted_iota(jnp.int32, (SLICE, TOKENS), 0)
-    embed = jnp.zeros((SLICE, 256), f32)
-    for m in range(8):
-        marks = (idsb[m, :1, :] == rows_).astype(f32).astype(bf16)
-        embed += jnp.dot(marks, bcot[m], preferred_element_type=f32)
-    tile_e[...] = embed.reshape(REPLICAS, 8, 256)
-
-    blocks = [column_block(z, xl, c, part) for part in range(2)]
-
-    def embed_copy(target, part):
-        cols = pl.ds(pl.multiple_of(blocks[part] * 128, 128), 128)
-        return tile_e.at[target, :, pl.ds(part * 128, 128)], er.at[z % 4, :, cols]
-
-    def send_embed(k, carry):
-        target = (replica + k) % REPLICAS
-        for part in range(2):
-            src, dst = embed_copy(target, part)
-            remote(src, dst, es.at[0], erv.at[0], (section, target)).start()
-        return carry
-
-    lax.fori_loop(1, REPLICAS, send_embed, 0)
-    for part in range(2):
-        src, dst = embed_copy(replica, part)
-        pltpu.make_async_copy(src, dst, erv.at[0]).start()
-
-    for copy in log_group:
+    for copy in log_core:
         copy.wait_recv()
     for j, copy in hid_all:
         if j == 0:
@@ -388,38 +455,42 @@
         else:
             copy.wait_recv()
 
-    head = jnp.zeros((SLICE, 512), f32)
-    for n in range(4):
-        head += dot(alog[n], bhid[n], TN)
-    tile_h[...] = head.reshape(REPLICAS, 8, 512)
-    head_cols = pl.ds(pl.multiple_of((xl * 2 + c) * 512, 512), 512)
+    head = jnp.zeros((SLICE, 256), f32)
+    for m in range(8):
+        head += dot(alog[m], bhid[m], TN)
+    tile_h[...] = head.reshape(REPLICAS, 8, 256)
+    head_block = (z // 4) * 4 + xl * 2 + c
+    head_cols = pl.ds(pl.multiple_of(head_block * 256, 256), 256)
 
     def send_head(k, carry):
         target = (replica + k) % REPLICAS
-        remote(tile_h.at[target], hr.at[z, :, head_cols], zs.at[0], zr.at[0], (section, target)).start()
+        remote(
+            tile_h.at[target], hr.at[z % 4, :, head_cols], zs.at[0], zr.at[0], (section, target)
+        ).start()
         return carry
 
     lax.fori_loop(1, REPLICAS, send_head, 0)
-    pltpu.make_async_copy(tile_h.at[replica], hr.at[z, :, head_cols], zr.at[0]).start()
+    pltpu.make_async_copy(tile_h.at[replica], hr.at[z % 4, :, head_cols], zr.at[0]).start()
 
     @pl.when(c == 1)
     def _():
-        near_copy.wait_recv()
-
-    for slot in range(3):
-        far_copy(1, slot, 0).wait_recv()
+        for h in range(2):
+            near_copy(h).wait_recv()
+
+    for h in range(2):
+        for slot in range(3):
+            far_copy(1, slot, 0, h).wait_recv()
     out_grad[...] = (
         rs0[...] + rs[0].astype(f32) + rs[1].astype(f32) + rs[2].astype(f32)
     )
     pltpu.make_async_copy(er, er, erv.at[0]).wait()
     embed_grad[...] = er[0] + er[1] + er[2] + er[3]
     pltpu.make_async_copy(hr, hr, zr.at[0]).wait()
-    total = hr[0]
-    for k in range(1, 8):
-        total += hr[k]
-    head_grad[...] = total
-
-    for copy in head_sends + forwards + mix_core + ids_sends + log_group + [mix_xl, mix_z, mix_diag]:
+    head_grad[...] = hr[0] + hr[1] + hr[2] + hr[3]
+
+    copies = [mix_xl, *head_sends.values(), *forwards.values()]
+    copies += mix_core + mix_z + mix_diag + core_z + core_diag + ids_sends + log_far + log_core
+    for copy in copies:
         copy.wait_send()
     for copies in (hid_sends, log_sends):
         for copy in copies[1:]:
@@ -437,15 +508,17 @@
 
     @pl.when(c == 0)
     def _():
-        far_copy(1, 1, 0).wait_send()
-        far_copy(1, 1, 1).wait_send()
-        near_copy.wait_send()
+        for h in range(2):
+            far_copy(1, 1, 0, h).wait_send()
+            far_copy(1, 1, 1, h).wait_send()
+            near_copy(h).wait_send()
 
     @pl.when(c == 1)
     def _():
-        for part in range(2):
-            for c_ in range(2):
-                far_copy(part, 0, c_).wait_send()
+        for h in range(2):
+            for part in range(2):
+                for c_ in range(2):
+                    far_copy(part, 0, c_, h).wait_send()
 
     sent = tile_e.at[pl.ds(0, REPLICAS - 1)]
     pltpu.make_async_copy(sent, sent, es.at[0]).wait()
@@ -453,7 +526,7 @@
     pltpu.make_async_copy(sent, sent, zs.at[0]).wait()
 
 
-def gradients(wide, mixed, head, weight, gain, targets, ids):
+def gradients(wide, mixed, head, weight, gain, target_ids, token_ids):
     dma = pltpu.SemaphoreType.DMA
     vm = pltpu.VMEM
     any_ = pl.BlockSpec(memory_space=pl.ANY)
@@ -483,38 +556,40 @@
             vm((BLOCK, WIDTH), bf16),
             vm((8, BLOCK, 256), bf16),
             vm((8, TOKENS, 256), bf16),
-            vm((4, BLOCK, 512), bf16),
-            vm((4, TOKENS, 512), bf16),
-            vm((4, TOKENS, SLICE), bf16),
+            vm((8, BLOCK, 256), bf16),
+            vm((8, TOKENS, 256), bf16),
+            vm((8, TOKENS, SLICE), bf16),
             vm((8, 8, TOKENS), jnp.int32),
+            vm((1, WIDTH), f32),
             vm((256, WIDTH), f32),
             vm((256, WIDTH), bf16),
             vm((3, OWNED, WIDTH), bf16),
             vm((OWNED, WIDTH), f32),
             vm((REPLICAS, 8, 256), f32),
-            vm((REPLICAS, 8, 512), f32),
+            vm((REPLICAS, 8, 256), f32),
             vm((4, 8, WIDTH), f32),
-            vm((8, 8, WIDTH), f32),
+            vm((4, 8, WIDTH), f32),
             dma((12,)),
             dma((8,)), dma((8,)),
             dma((8,)), dma((8,)),
             dma((8,)), dma((8,)),
-            dma((4,)), dma((4,)),
+            dma((8,)), dma((8,)),
             dma((2, 8)), dma((2,)),
             dma((8,)), dma((8,)),
             dma((8, 2)), dma((8, 2)),
             dma((8,)), dma((8,)),
             dma((8,)), dma((8,)),
-            dma((4,)), dma((4,)),
-            dma((8,)), dma((8,)),
-            dma((2, 2)), dma((4,)),
+            dma((8,)), dma((8,)),
+            dma((8,)), dma((8,)),
+            dma((2, 2, 2)), dma((2, 4)),
             dma((1,)), dma((1,)),
             dma((1,)), dma((1,)),
+            dma((4, 4)), dma((4, 4)),
         ],
         compiler_params=pltpu.CompilerParams(
             collective_id=0, has_side_effects=True, vmem_limit_bytes=60 * 2**20
         ),
-    )(wide, mixed, head, weight, gain, targets, ids)
+    )(wide, mixed, head, weight, gain, target_ids, token_ids)
 
 
 def adam_update(master, first, second, gradient):
@@ -531,17 +606,14 @@
     out_master, out_first, out_second, head_master, head_first, head_second,
     embed_master, embed_first, embed_second,
 ):
-    section = lax.axis_index("section")
-    targets = lax.dynamic_slice_in_dim(target_ids.reshape(TOKENS, 1), section * BLOCK, BLOCK, 0)
-    ids = jnp.broadcast_to(token_ids.reshape(1, TOKENS), (8, TOKENS))
     out_gradient, head_gradient, embed_gradient = gradients(
         block_inputs.reshape(TOKENS, WIDTH),
         mixed_inputs.reshape(TOKENS, WIDTH),
         head_weight,
         out_weight.reshape(WIDTH, WIDTH),
-        final_gain.reshape(1, WIDTH),
-        targets,
-        ids,
+        final_gain,
+        target_ids,
+        token_ids,
     )
     return (
         *adam_update(out_master, out_first, out_second, out_gradient.reshape(out_master.shape)),

time: 171 us -> 134 us (0.78)
  the two profiles are of different devices: /device:TPU:7 before, /device:TPU:29 now
where the time goes in v2:
time: 134 us; the launch traced here: 133 us
  Pallas kernels  129 us (96%)
  other arithmetic  4.04 us (3%)
    pallas_call x1, Pallas kernels, gradients(): pl.pallas_call(kernel, out_shape=(jax.ShapeDtypeStruct((OWNED, WIDTH), f3...  129 us
    sub x2, other arithmetic, adam_update(): master - learning_rate * (first_next / (jnp.sqrt(second_next) + adam_eps)...  4.04 us

profile of v2, /device:TPU:29, one launch (start us, length us, event | category | flops | bytes accessed | tf_op | source)
XLA Modules:
  0.0 133.5 jit_solution(5493119212102318769)
XLA Ops:
  0.6 0.0 copy-start
  0.7 0.0 copy-start.1
  0.7 0.0 copy-start.2
  0.7 0.0 copy-start.3
  0.7 0.0 copy-start.4
  0.7 0.0 copy-start.5
  0.7 0.0 copy-start.6
  0.7 0.0 copy-start.7
  0.7 0.0 copy-start.8
  0.7 128.6 %shard_map.223 = (f32[64,2048]{1,0:T(8,128)}, f32[8,2048]{1,0:T(8,128)}, f32[8,2048]{1,0:T(8,128)}) custom-call(bf16[256,2048]{1,0:T(8,128)(2,1)} %bitcast.12, bf16[256,2048]{1,0:T(8,128)(2,1)} %bitcast.13, bf16[256,2048]{1,0:T(8,128)(2,1)} %head_hbm.1, bf16[2048,2048]{1,0:T(8,128)(2,1)} %bitcast.11, f32[2048]{0:T(1024)} %gain_in.1, s32[4,64]{1,0:T(4,128)} %target_ids.1, ...), custom_call_target="tpu_custom_call" | custom-call | tf_op jit(solution)/shard_map/pallas_call | solution.py:534
  129.4 0.0 copy-done
  129.4 0.0 copy-done.1
  129.4 0.0 copy-done.2
  129.4 2.4 %multiply_subtract_fusion = (f32[1,64,2048]{2,1,0:T(8,128)}, f32[1,64,2048]{2,1,0:T(8,128)}, f32[1,64,2048]{2,1,0:T(8,128)}) fusion(f32[1,64,2048]{2,1,0:T(8,128)S(1)} %copy-done, f32[64,2048]{1,0:T(8,128)} %get-tuple-element.12, f32[1,64,2048]{2,1,0:T(8,128)S(1)} %copy-done.1, f32[1,64,2048]{2,1,0:T(8,128)S(1)} %copy-done.2), kind=kLoop, calls=%fused_computation.4 | loop fusion | flops 1703936 | bytes 3670016 | tf_op jit(solution)/shard_map/sub | solution.py:598
  131.8 0.0 copy-done.3
  131.8 0.0 copy-done.4
  131.8 0.0 copy-done.5
  131.8 0.0 copy-done.6
  131.8 0.0 copy-done.7
  131.8 0.0 copy-done.8
  131.8 1.7 %multiply_subtract_fusion.1 = (f32[8,2048]{1,0:T(8,128)}, f32[8,2048]{1,0:T(8,128)}, f32[8,2048]{1,0:T(8,128)}, f32[8,2048]{1,0:T(8,128)}, f32[8,2048]{1,0:T(8,128)}, /*index=5*/f32[8,2048]{1,0:T(8,128)}) fusion(f32[8,2048]{1,0:T(8,128)S(1)} %copy-done.3, f32[8,2048]{1,0:T(8,128)} %get-tuple-element.14, f32[8,2048]{1,0:T(8,128)S(1)} %copy-done.4, ...), kind=kLoop, calls=%fused_computation.9 | loop fusion | flops 425984 | bytes 917504 | tf_op jit(solution)/shard_map/sub | solution.py:598
Async XLA Ops:
  0.6 128.7 %copy-start = (f32[1,64,2048]{2,1,0:T(8,128)S(1)}, f32[1,64,2048]{2,1,0:T(8,128)}, u32[]{:S(2)}) copy-start(f32[1,64,2048]{2,1,0:T(8,128)} %param.23) | copy-start | bytes 1572868
  0.7 128.7 %copy-start.1 = (f32[1,64,2048]{2,1,0:T(8,128)S(1)}, f32[1,64,2048]{2,1,0:T(8,128)}, u32[]{:S(2)}) copy-start(f32[1,64,2048]{2,1,0:T(8,128)} %param.25) | copy-start | bytes 1572868
  0.7 128.7 %copy-start.2 = (f32[1,64,2048]{2,1,0:T(8,128)S(1)}, f32[1,64,2048]{2,1,0:T(8,128)}, u32[]{:S(2)}) copy-start(f32[1,64,2048]{2,1,0:T(8,128)} %param.24) | copy-start | bytes 1572868
  0.7 131.1 %copy-start.3 = (f32[8,2048]{1,0:T(8,128)S(1)}, f32[8,2048]{1,0:T(8,128)}, u32[]{:S(2)}) copy-start(f32[8,2048]{1,0:T(8,128)} %param.29) | copy-start | bytes 196612
  0.7 131.1 %copy-start.4 = (f32[8,2048]{1,0:T(8,128)S(1)}, f32[8,2048]{1,0:T(8,128)}, u32[]{:S(2)}) copy-start(f32[8,2048]{1,0:T(8,128)} %param.31) | copy-start | bytes 196612
  0.7 131.1 %copy-start.5 = (f32[8,2048]{1,0:T(8,128)S(1)}, f32[8,2048]{1,0:T(8,128)}, u32[]{:S(2)}) copy-start(f32[8,2048]{1,0:T(8,128)} %param.30) | copy-start | bytes 196612
  0.7 131.1 %copy-start.6 = (f32[8,2048]{1,0:T(8,128)S(1)}, f32[8,2048]{1,0:T(8,128)}, u32[]{:S(2)}) copy-start(f32[8,2048]{1,0:T(8,128)} %param.26) | copy-start | bytes 196612
  0.7 131.1 %copy-start.7 = (f32[8,2048]{1,0:T(8,128)S(1)}, f32[8,2048]{1,0:T(8,128)}, u32[]{:S(2)}) copy-start(f32[8,2048]{1,0:T(8,128)} %param.28) | copy-start | bytes 196612
  0.7 131.1 %copy-start.8 = (f32[8,2048]{1,0:T(8,128)S(1)}, f32[8,2048]{1,0:T(8,128)}, u32[]{:S(2)}) copy-start(f32[8,2048]{1,0:T(8,128)} %param.27) | copy-start | bytes 196612

commit v3 on v2

--- a/solution.py
+++ b/solution.py
@@ -60,6 +60,13 @@
         kz, kl, kc = m // 4, (m // 2) % 2, m % 2
         return (z + 4 * kz) % 8, flip(xl, kl), flip(c, kc)
 
+    def head_member(m):
+        near = (z + (m // 2) % 2 * (1 - 2 * (z % 2))) % 8
+        return (near + 4 * (m // 4)) % 8, xl, flip(c, m % 2)
+
+    def head_column(z_, c_):
+        return (z_ // 4) * 4 + (z_ % 2) * 2 + c_
+
     def remote(src, dst, send, recv, device):
         return pltpu.make_async_remote_copy(
             src_ref=src, dst_ref=dst, send_sem=send, recv_sem=recv,
@@ -100,13 +107,21 @@
     def sender_slice(j):
         return y_peer(y, j // 2) * 2 + flip(xh, j % 2)
 
+    HALVES = ((0, 64), (64, 128))
     head_sends = {}
 
-    def head_send(slot, source, peer):
-        part = hd.at[sender_slice(source), half]
-        copy = remote(part, part, hs.at[slot], hrv.at[slot], section_peer(peer, True))
-        copy.start()
-        head_sends[slot] = copy
+    def head_copy(slot, source, peer, rows=(0, 128)):
+        first, last = rows
+        part = hd.at[
+            sender_slice(source), pl.ds(pl.multiple_of(c * 128 + first, 16), last - first)
+        ]
+        lane = int(first > 0)
+        return remote(part, part, hs.at[lane, slot], hrv.at[lane, slot], section_peer(peer, True))
+
+    def head_send(slot, source, peer, rows=(0, 128)):
+        copy = head_copy(slot, source, peer, rows)
+        copy.start()
+        head_sends[slot, rows] = copy
 
     load_head.wait()
     for j in (1, 2, 6):
@@ -117,13 +132,19 @@
     def mix_copy(src, dst, device):
         return remote(mix.at[src], mix.at[dst], ms.at[dst], mr.at[dst], device)
 
-    mix_xl = mix_copy(0, 2, dev(y, xh, z, 1 - xl, c))
+    mix_xl = [
+        remote(
+            mix.at[0, pl.ds(h * 128, 128)], mix.at[2, pl.ds(h * 128, 128)],
+            fms.at[1 + h, 0], fmr.at[1 + h, 0], dev(y, xh, z, 1 - xl, c),
+        )
+        for h in range(2)
+    ]
     mix_core = [mix_copy(m, m + 1, partner) for m in (0, 2)]
 
     def far_mix(src, dst, device):
         rows = [pl.ds(k * 64, 64) for k in range(4)]
         return [
-            remote(mix.at[src, r], mix.at[dst, r], fms.at[dst - 4, k], fmr.at[dst - 4, k], device)
+            remote(mix.at[src, r], mix.at[dst, r], fms.at[dst, k], fmr.at[dst, k], device)
             for k, r in enumerate(rows)
         ]
 
@@ -131,8 +152,9 @@
     mix_diag = far_mix(4, 6, dev(y, xh, z, 1 - xl, c))
     core_z = far_mix(4, 5, partner)
     core_diag = far_mix(6, 7, partner)
-    for copy in mix_z:
-        copy.start()
+    mix_z[0].start()
+    mix_z[1].start()
+    mix_xl[0].start()
     mix_core[0].start()
     idsb[0] = jnp.broadcast_to(
         jnp.concatenate([token_ids[b : b + 1, :] for b in range(4)], axis=1), (8, TOKENS)
@@ -181,14 +203,20 @@
         hmine[...] = hid[(SECTIONS - 1) * BLOCK :, :]
         smine[...] = stats[(SECTIONS - 1) * BLOCK :, :]
 
-    head_send(4, 0, 4)
-    mix_xl.start()
+    for rows in HALVES:
+        head_send(4, 0, 4, rows)
+    mix_xl[1].start()
 
     forwards = {}
+
+    SPLIT = ((0, 112), (112, 128))
 
     def pass_on(j):
         part = hd.at[sender_slice(j), half]
-        remote(part, part, hs.at[j], hrv.at[j], section_peer(j, True)).wait_recv()
+        for rows in {3: SPLIT, 7: SPLIT, 4: HALVES, 5: HALVES}.get(j, ((0, 128),)):
+            head_copy(j, j, j, rows).wait_recv()
+            if j == 4:
+                head_send(5, 4, 1, rows)
         copy = remote(part, part, fs.at[j], fr.at[j], partner)
         copy.start()
         forwards[j] = copy
@@ -197,26 +225,29 @@
         mix_z[k].wait_recv()
         mix_diag[k].start()
         core_z[k].start()
+        if k == 0:
+            mix_z[2].start()
 
     pass_on(1)
-    head_send(3, 1, 2)
-    head_send(7, 1, 6)
+    head_send(3, 1, 2, SPLIT[0])
+    head_send(7, 1, 6, SPLIT[0])
     pass_on(2)
+    head_send(3, 2, 1, SPLIT[1])
     pass_on(6)
+    head_send(7, 6, 1, SPLIT[1])
     pass_far(0)
     pass_on(4)
-    head_send(5, 4, 1)
-    pass_far(1)
 
     @pl.when(jnp.logical_not(root))
     def _():
         for copy in hidden_send(1):
             copy.wait_recv()
 
+    mine = pl.ds(pl.multiple_of(section * BLOCK, BLOCK), BLOCK)
     hid_sends = []
     for m in range(8):
-        z_, xl_, c_ = member(m)
-        block = (z_ // 4) * 4 + xl_ * 2 + c_
+        z_, xl_, c_ = head_member(m)
+        block = head_column(z_, c_)
         src = hmine.at[:, pl.ds(pl.multiple_of(block * 256, 256), 256)]
         if m == 0:
             copy = pltpu.make_async_copy(src, ghid.at[0], nr.at[0])
@@ -224,18 +255,20 @@
             copy = remote(src, ghid.at[m], ns.at[m], nr.at[m], dev(y, xh, z_, xl_, c_))
         copy.start()
         hid_sends.append(copy)
+    mix_z[3].start()
 
     def logits(j):
         n = sender_slice(j)
         lg[:, pl.ds(pl.multiple_of(n * SLICE, SLICE), SLICE)] = dot(hmine[...], hd[n], NT)
 
-    logits(0)
-    for j in (1, 2, 6, 4):
-        forwards[j].wait_recv()
+    for j in (0, 1, 2, 6):
+        if j:
+            forwards[j].wait_recv()
         logits(j)
+    pass_far(1)
     for j in (3, 7, 5):
         pass_on(j)
-    for j in (3, 7, 5):
+    for j in (4, 3, 7, 5):
         forwards[j].wait_recv()
         logits(j)
     values = lg[...]
@@ -250,7 +283,6 @@
     )
     lcb[...] = jnp.where(targets == columns_.astype(f32), predicted - 1.0, predicted).astype(bf16)
 
-    mine = pl.ds(pl.multiple_of(section * BLOCK, BLOCK), BLOCK)
     log_sends = []
     for j in range(8):
         peer_section = sender_slice(j)
@@ -263,8 +295,28 @@
         copy.start()
         log_sends.append(copy)
 
-    pass_far(2)
-
+    def block_rows(j):
+        return pl.ds(pl.multiple_of(sender_slice(j) * BLOCK, BLOCK), BLOCK)
+
+    for n, copy in enumerate(hid_sends):
+        if n == 0:
+            copy.wait()
+        else:
+            copy.wait_recv()
+
+    hid_all = {}
+
+    def gather_hidden(slot, src, rows, peer):
+        dst = bhid.at[:, rows]
+        if slot == 0:
+            copy = pltpu.make_async_copy(src, dst, wr.at[0])
+        else:
+            copy = remote(src, dst, ws.at[slot], wr.at[slot], section_peer(peer))
+        copy.start()
+        hid_all[slot] = copy
+
+    for j in (2, 6, 4, 0):
+        gather_hidden(j, ghid, mine, j)
     def back(n, carry):
         cols = pl.ds(pl.multiple_of(n * 256, 256), 256)
         total = jnp.zeros((BLOCK, 256), f32)
@@ -304,44 +356,40 @@
             copy.start()
             cot_sends.append((m, copy))
 
+    cot_all = {}
+
+    def gather_cotangent(slot, part, src, rows, peer):
+        members = pl.ds(part * 4, 4)
+        dst = bcot.at[members, rows]
+        if slot == 0:
+            copy = pltpu.make_async_copy(src.at[members], dst, cr.at[part, 0])
+        else:
+            copy = remote(
+                src.at[members, rows] if src is bcot else src.at[members],
+                dst, cs.at[part, slot], cr.at[part, slot], section_peer(peer),
+            )
+        copy.start()
+        cot_all[slot, part] = copy
+
+    for part in range(2):
+        for m, copy in cot_sends:
+            if m // 4 == part:
+                copy.wait() if m == 0 else copy.wait_recv()
+        for j in (1, 2, 6, 4, 0):
+            gather_cotangent(j, part, gcot, mine, j)
+
+    pass_far(2)
+    for part in range(2):
+        cot_all[1, part].wait_recv()
+        for j in (2, 6, 4):
+            gather_cotangent(j + 1, part, bcot, block_rows(1), j)
+
     pass_far(3)
-    mix_xl.wait_recv()
-    mix_core[1].start()
-
-    for n, copy in enumerate(hid_sends):
-        if n == 0:
-            copy.wait()
-        else:
-            copy.wait_recv()
-    hid_all = []
-
-    def gather_hidden(j):
-        dst = bhid.at[:, mine]
-        if j == 0:
-            copy = pltpu.make_async_copy(ghid, dst, wr.at[0])
-        else:
-            copy = remote(ghid, dst, ws.at[j], wr.at[j], section_peer(j))
-        copy.start()
-        hid_all.append((j, copy))
-
-    for j in (2, 6, 4, 0):
-        gather_hidden(j)
-
-    for m, copy in cot_sends:
-        if m == 0:
-            copy.wait()
-        else:
-            copy.wait_recv()
-    all_sends = []
-    for j in (6, 7, 4, 5, 1, 2, 3, 0):
-        dst = bcot.at[:, mine]
-        if j == 0:
-            copy = pltpu.make_async_copy(gcot, dst, cr.at[0])
-        else:
-            copy = remote(gcot, dst, cs.at[j], cr.at[j], section_peer(j))
-        copy.start()
-        all_sends.append((j, copy))
-
+    hid_all[0].wait()
+    for j in (2, 6, 4):
+        hid_all[j].wait_recv()
+    for j in (0, 2, 6, 4):
+        gather_hidden(j + 1, bhid.at[:, block_rows(j)], block_rows(j), 1)
     for j, copy in enumerate(log_sends):
         if j == 0:
             copy.wait()
@@ -350,29 +398,25 @@
     def log_copy(src, dst, device):
         return remote(alog.at[src], alog.at[dst], vs.at[dst], vr.at[dst], device)
 
-    log_far = [log_copy(0, m, dev(y, xh, *member(m))) for m in (4, 6, 2)]
+    log_far = [log_copy(0, m, dev(y, xh, *head_member(m))) for m in (4, 6, 2)]
     log_core = [log_copy(m, m + 1, partner) for m in (0, 2, 4, 6)]
     for copy in log_far + log_core[:1]:
         copy.start()
-    for j in (3, 7, 5, 1):
-        gather_hidden(j)
-
+
+    for h in range(2):
+        mix_xl[h].wait_recv()
+    mix_core[1].start()
     for k in range(4):
         mix_diag[k].wait_recv()
         core_diag[k].start()
     for copy in mix_core + core_z + core_diag:
         copy.wait_recv()
-    for copy in log_far:
-        copy.wait_recv()
-    for copy in log_core[1:]:
-        copy.start()
     for copy in ids_sends:
         copy.wait_recv()
-    for j, copy in all_sends:
-        if j == 0:
-            copy.wait()
-        else:
-            copy.wait_recv()
+    for part in range(2):
+        cot_all[0, part].wait()
+        for j in (2, 6, 4, 3, 7, 5):
+            cot_all[j, part].wait_recv()
 
     rows_ = section * SLICE + lax.broadcasted_iota(jnp.int32, (SLICE, TOKENS), 0)
     embed = jnp.zeros((SLICE, 256), f32)
@@ -447,30 +491,31 @@
     def _():
         rs0[...] = psum[:OWNED, :]
 
+    for copy in log_far:
+        copy.wait_recv()
+    for copy in log_core[1:]:
+        copy.start()
     for copy in log_core:
         copy.wait_recv()
-    for j, copy in hid_all:
-        if j == 0:
-            copy.wait()
-        else:
-            copy.wait_recv()
+    for j in (1, 3, 7, 5):
+        hid_all[j].wait_recv()
 
     head = jnp.zeros((SLICE, 256), f32)
     for m in range(8):
         head += dot(alog[m], bhid[m], TN)
     tile_h[...] = head.reshape(REPLICAS, 8, 256)
-    head_block = (z // 4) * 4 + xl * 2 + c
-    head_cols = pl.ds(pl.multiple_of(head_block * 256, 256), 256)
+    head_cols = pl.ds(pl.multiple_of(head_column(z, c) * 256, 256), 256)
+    head_class = xl * 2 + (z // 2) % 2
 
     def send_head(k, carry):
         target = (replica + k) % REPLICAS
         remote(
-            tile_h.at[target], hr.at[z % 4, :, head_cols], zs.at[0], zr.at[0], (section, target)
+            tile_h.at[target], hr.at[head_class, :, head_cols], zs.at[0], zr.at[0], (section, target)
         ).start()
         return carry
 
     lax.fori_loop(1, REPLICAS, send_head, 0)
-    pltpu.make_async_copy(tile_h.at[replica], hr.at[z % 4, :, head_cols], zr.at[0]).start()
+    pltpu.make_async_copy(tile_h.at[replica], hr.at[head_class, :, head_cols], zr.at[0]).start()
 
     @pl.when(c == 1)
     def _():
@@ -488,17 +533,18 @@
     pltpu.make_async_copy(hr, hr, zr.at[0]).wait()
     head_grad[...] = hr[0] + hr[1] + hr[2] + hr[3]
 
-    copies = [mix_xl, *head_sends.values(), *forwards.values()]
+    copies = [*mix_xl, *head_sends.values(), *forwards.values()]
+    copies += [cot_all[j, part] for j in range(1, 8) for part in range(2)]
+    copies += [hid_all[j] for j in range(1, 8)]
     copies += mix_core + mix_z + mix_diag + core_z + core_diag + ids_sends + log_far + log_core
     for copy in copies:
         copy.wait_send()
     for copies in (hid_sends, log_sends):
         for copy in copies[1:]:
             copy.wait_send()
-    for copies in (cot_sends, all_sends, hid_all):
-        for index, copy in copies:
-            if index:
-                copy.wait_send()
+    for m, copy in cot_sends:
+        if m:
+            copy.wait_send()
 
     @pl.when(root)
     def _():
@@ -570,21 +616,21 @@
             vm((4, 8, WIDTH), f32),
             vm((4, 8, WIDTH), f32),
             dma((12,)),
-            dma((8,)), dma((8,)),
+            dma((2, 8)), dma((2, 8)),
             dma((8,)), dma((8,)),
             dma((8,)), dma((8,)),
             dma((8,)), dma((8,)),
             dma((2, 8)), dma((2,)),
             dma((8,)), dma((8,)),
             dma((8, 2)), dma((8, 2)),
-            dma((8,)), dma((8,)),
+            dma((2, 8)), dma((2, 8)),
             dma((8,)), dma((8,)),
             dma((8,)), dma((8,)),
             dma((8,)), dma((8,)),
             dma((2, 2, 2)), dma((2, 4)),
             dma((1,)), dma((1,)),
             dma((1,)), dma((1,)),
-            dma((4, 4)), dma((4, 4)),
+            dma((8, 4)), dma((8, 4)),
         ],
         compiler_params=pltpu.CompilerParams(
             collective_id=0, has_side_effects=True, vmem_limit_bytes=60 * 2**20

time: 134 us -> 120 us (0.90)
  the two profiles are of different devices: /device:TPU:29 before, /device:TPU:7 now
where the time goes in v3:
time: 120 us
  Pallas kernels  115 us (96%)
  other arithmetic  4.04 us (3%)
    pallas_call x1, Pallas kernels, gradients(): pl.pallas_call(kernel, out_shape=(jax.ShapeDtypeStruct((OWNED, WIDTH), f3...  115 us
    sub x2, other arithmetic, adam_update(): master - learning_rate * (first_next / (jnp.sqrt(second_next) + adam_eps)...  4.04 us

profile of v3, /device:TPU:7, one launch (start us, length us, event | category | flops | bytes accessed | tf_op | source)
XLA Modules:
  0.0 119.6 jit_solution(7617457172846066733)
XLA Ops:
  0.6 0.0 copy-start
  0.7 0.0 copy-start.1
  0.7 0.0 copy-start.2
  0.7 0.0 copy-start.3
  0.7 0.0 copy-start.4
  0.7 0.0 copy-start.5
  0.7 0.0 copy-start.6
  0.7 0.0 copy-start.7
  0.7 0.0 copy-start.8
  0.7 114.7 %shard_map.223 = (f32[64,2048]{1,0:T(8,128)}, f32[8,2048]{1,0:T(8,128)}, f32[8,2048]{1,0:T(8,128)}) custom-call(bf16[256,2048]{1,0:T(8,128)(2,1)} %bitcast.12, bf16[256,2048]{1,0:T(8,128)(2,1)} %bitcast.13, bf16[256,2048]{1,0:T(8,128)(2,1)} %head_hbm.1, bf16[2048,2048]{1,0:T(8,128)(2,1)} %bitcast.11, f32[2048]{0:T(1024)} %gain_in.1, s32[4,64]{1,0:T(4,128)} %target_ids.1, ...), custom_call_target="tpu_custom_call" | custom-call | tf_op jit(solution)/shard_map/pallas_call | solution.py:580
  115.4 0.0 copy-done
  115.5 0.0 copy-done.1
  115.5 0.0 copy-done.2
  115.5 2.4 %multiply_subtract_fusion = (f32[1,64,2048]{2,1,0:T(8,128)}, f32[1,64,2048]{2,1,0:T(8,128)}, f32[1,64,2048]{2,1,0:T(8,128)}) fusion(f32[1,64,2048]{2,1,0:T(8,128)S(1)} %copy-done, f32[64,2048]{1,0:T(8,128)} %get-tuple-element.12, f32[1,64,2048]{2,1,0:T(8,128)S(1)} %copy-done.1, f32[1,64,2048]{2,1,0:T(8,128)S(1)} %copy-done.2), kind=kLoop, calls=%fused_computation.4 | loop fusion | flops 1703936 | bytes 3670016 | tf_op jit(solution)/shard_map/sub | solution.py:644
  117.9 0.0 copy-done.3
  117.9 0.0 copy-done.4
  117.9 0.0 copy-done.5
  117.9 0.0 copy-done.6
  117.9 0.0 copy-done.7
  117.9 0.0 copy-done.8
  117.9 1.7 %multiply_subtract_fusion.1 = (f32[8,2048]{1,0:T(8,128)}, f32[8,2048]{1,0:T(8,128)}, f32[8,2048]{1,0:T(8,128)}, f32[8,2048]{1,0:T(8,128)}, f32[8,2048]{1,0:T(8,128)}, /*index=5*/f32[8,2048]{1,0:T(8,128)}) fusion(f32[8,2048]{1,0:T(8,128)S(1)} %copy-done.3, f32[8,2048]{1,0:T(8,128)} %get-tuple-element.14, f32[8,2048]{1,0:T(8,128)S(1)} %copy-done.4, ...), kind=kLoop, calls=%fused_computation.9 | loop fusion | flops 425984 | bytes 917504 | tf_op jit(solution)/shard_map/sub | solution.py:644
Async XLA Ops:
  0.6 114.8 %copy-start = (f32[1,64,2048]{2,1,0:T(8,128)S(1)}, f32[1,64,2048]{2,1,0:T(8,128)}, u32[]{:S(2)}) copy-start(f32[1,64,2048]{2,1,0:T(8,128)} %param.23) | copy-start | bytes 1572868
  0.7 114.8 %copy-start.1 = (f32[1,64,2048]{2,1,0:T(8,128)S(1)}, f32[1,64,2048]{2,1,0:T(8,128)}, u32[]{:S(2)}) copy-start(f32[1,64,2048]{2,1,0:T(8,128)} %param.25) | copy-start | bytes 1572868
  0.7 114.8 %copy-start.2 = (f32[1,64,2048]{2,1,0:T(8,128)S(1)}, f32[1,64,2048]{2,1,0:T(8,128)}, u32[]{:S(2)}) copy-start(f32[1,64,2048]{2,1,0:T(8,128)} %param.24) | copy-start | bytes 1572868
  0.7 117.2 %copy-start.3 = (f32[8,2048]{1,0:T(8,128)S(1)}, f32[8,2048]{1,0:T(8,128)}, u32[]{:S(2)}) copy-start(f32[8,2048]{1,0:T(8,128)} %param.29) | copy-start | bytes 196612
  0.7 117.2 %copy-start.4 = (f32[8,2048]{1,0:T(8,128)S(1)}, f32[8,2048]{1,0:T(8,128)}, u32[]{:S(2)}) copy-start(f32[8,2048]{1,0:T(8,128)} %param.31) | copy-start | bytes 196612
  0.7 117.2 %copy-start.5 = (f32[8,2048]{1,0:T(8,128)S(1)}, f32[8,2048]{1,0:T(8,128)}, u32[]{:S(2)}) copy-start(f32[8,2048]{1,0:T(8,128)} %param.30) | copy-start | bytes 196612
  0.7 117.2 %copy-start.6 = (f32[8,2048]{1,0:T(8,128)S(1)}, f32[8,2048]{1,0:T(8,128)}, u32[]{:S(2)}) copy-start(f32[8,2048]{1,0:T(8,128)} %param.26) | copy-start | bytes 196612
  0.7 117.2 %copy-start.7 = (f32[8,2048]{1,0:T(8,128)S(1)}, f32[8,2048]{1,0:T(8,128)}, u32[]{:S(2)}) copy-start(f32[8,2048]{1,0:T(8,128)} %param.28) | copy-start | bytes 196612
  0.7 117.2 %copy-start.8 = (f32[8,2048]{1,0:T(8,128)S(1)}, f32[8,2048]{1,0:T(8,128)}, u32[]{:S(2)}) copy-start(f32[8,2048]{1,0:T(8,128)} %param.27) | copy-start | bytes 196612

commit v4 on v3

--- a/solution.py
+++ b/solution.py
@@ -315,7 +315,7 @@
         copy.start()
         hid_all[slot] = copy
 
-    for j in (2, 6, 4, 0):
+    for j in (1, 2, 6, 4, 0):
         gather_hidden(j, ghid, mine, j)
     def back(n, carry):
         cols = pl.ds(pl.multiple_of(n * 256, 256), 256)
@@ -385,11 +385,9 @@
             gather_cotangent(j + 1, part, bcot, block_rows(1), j)
 
     pass_far(3)
-    hid_all[0].wait()
+    hid_all[1].wait_recv()
     for j in (2, 6, 4):
-        hid_all[j].wait_recv()
-    for j in (0, 2, 6, 4):
-        gather_hidden(j + 1, bhid.at[:, block_rows(j)], block_rows(j), 1)
+        gather_hidden(j + 1, bhid.at[:, block_rows(1)], block_rows(1), j)
     for j, copy in enumerate(log_sends):
         if j == 0:
             copy.wait()
@@ -406,17 +404,36 @@
     for h in range(2):
         mix_xl[h].wait_recv()
     mix_core[1].start()
-    for k in range(4):
+    def pass_diag(k):
         mix_diag[k].wait_recv()
         core_diag[k].start()
-    for copy in mix_core + core_z + core_diag:
+
+    for k in range(3):
+        pass_diag(k)
+    for copy in mix_core:
+        copy.wait_recv()
+
+    def cotangent_part(part):
+        cot_all[0, part].wait()
+        for j in (2, 6, 4, 3, 7, 5):
+            cot_all[j, part].wait_recv()
+
+    def near_product(n, carry):
+        cols = pl.ds(pl.multiple_of(n * 256, 256), 256)
+        total = jnp.zeros((256, 256), f32)
+        for m in range(4):
+            total += dot(bcot[m], mix[m, :, cols], TN)
+        psum[:, cols] = total
+        return carry
+
+    cotangent_part(0)
+    lax.fori_loop(0, WIDTH // 256, near_product, 0)
+    pass_diag(3)
+    for copy in core_z + core_diag:
         copy.wait_recv()
     for copy in ids_sends:
         copy.wait_recv()
-    for part in range(2):
-        cot_all[0, part].wait()
-        for j in (2, 6, 4, 3, 7, 5):
-            cot_all[j, part].wait_recv()
+    cotangent_part(1)
 
     rows_ = section * SLICE + lax.broadcasted_iota(jnp.int32, (SLICE, TOKENS), 0)
     embed = jnp.zeros((SLICE, 256), f32)
@@ -425,28 +442,20 @@
         embed += jnp.dot(marks, bcot[m], preferred_element_type=f32)
     tile_e[...] = embed.reshape(REPLICAS, 8, 256)
 
-    blocks = [column_block(z, xl, c, part) for part in range(2)]
-
-    def embed_copy(target, part):
-        cols = pl.ds(pl.multiple_of(blocks[part] * 128, 128), 128)
-        return tile_e.at[target, :, pl.ds(part * 128, 128)], er.at[z % 4, :, cols]
-
     def send_embed(k, carry):
         target = (replica + k) % REPLICAS
-        for part in range(2):
-            src, dst = embed_copy(target, part)
-            remote(src, dst, es.at[0], erv.at[0], (section, target)).start()
+        remote(
+            tile_e.at[target], er.at[replica], es.at[0], erv.at[0], (section, target)
+        ).start()
         return carry
 
     lax.fori_loop(1, REPLICAS, send_embed, 0)
-    for part in range(2):
-        src, dst = embed_copy(replica, part)
-        pltpu.make_async_copy(src, dst, erv.at[0]).start()
+    pltpu.make_async_copy(tile_e.at[replica], er.at[replica], erv.at[0]).start()
 
     def product(n, carry):
         cols = pl.ds(pl.multiple_of(n * 256, 256), 256)
-        total = jnp.zeros((256, 256), f32)
-        for m in range(8):
+        total = psum[:, cols]
+        for m in range(4, 8):
             total += dot(bcot[m], mix[m, :, cols], TN)
         psum[:, cols] = total
         psend[:, cols] = total.astype(bf16)
@@ -497,7 +506,8 @@
         copy.start()
     for copy in log_core:
         copy.wait_recv()
-    for j in (1, 3, 7, 5):
+    hid_all[0].wait()
+    for j in (2, 6, 4, 3, 7, 5):
         hid_all[j].wait_recv()
 
     head = jnp.zeros((SLICE, 256), f32)
@@ -529,7 +539,15 @@
         rs0[...] + rs[0].astype(f32) + rs[1].astype(f32) + rs[2].astype(f32)
     )
     pltpu.make_async_copy(er, er, erv.at[0]).wait()
-    embed_grad[...] = er[0] + er[1] + er[2] + er[3]
+    for block in range(16):
+        parts = [
+            er[z_ * 4 + block % 2 * 2 + c_, :, part * 128 : (part + 1) * 128]
+            for z_ in range(8)
+            for c_ in range(2)
+            for part in range(2)
+            if (z_ + (1 - 2 * (z_ % 2)) * ((0, 1), (-1, 2))[c_][part]) % 8 == block // 2
+        ]
+        embed_grad[:, block * 128 : (block + 1) * 128] = (parts[0] + parts[1]) + (parts[2] + parts[3])
     pltpu.make_async_copy(hr, hr, zr.at[0]).wait()
     head_grad[...] = hr[0] + hr[1] + hr[2] + hr[3]
 
@@ -613,7 +631,7 @@
             vm((OWNED, WIDTH), f32),
             vm((REPLICAS, 8, 256), f32),
             vm((REPLICAS, 8, 256), f32),
-            vm((4, 8, WIDTH), f32),
+            vm((REPLICAS, 8, 256), f32),
             vm((4, 8, WIDTH), f32),
             dma((12,)),
             dma((2, 8)), dma((2, 8)),
@@ -647,6 +665,40 @@
     return (master_next, first_next, second_next)
 
 
+def adam_kernel(*refs):
+    def update(k, rows):
+        gradient, master, first, second = (refs[4 * k + n][rows, :] for n in range(4))
+        results = adam_update(master, first, second, gradient)
+        for n in range(3):
+            refs[12 + 3 * k + n][rows, :] = results[n]
+
+    def chunk(i, carry):
+        update(0, pl.ds(pl.multiple_of(i * 8, 8), 8))
+        return carry
+
+    lax.fori_loop(0, refs[0].shape[0] // 8, chunk, 0)
+
+    @pl.when(pl.program_id(0) == 0)
+    def _():
+        update(1, slice(None))
+        update(2, slice(None))
+
+
+def adam(groups):
+    steps = 2
+    wide = pl.BlockSpec((OWNED // steps, WIDTH), lambda i: (i, 0))
+    narrow = pl.BlockSpec((8, WIDTH), lambda i: (0, 0))
+    specs = [wide] * 4 + [narrow] * 8
+    operands = [array for group in groups for array in group]
+    return pl.pallas_call(
+        adam_kernel,
+        out_shape=[jax.ShapeDtypeStruct(groups[k][0].shape, f32) for k in range(3) for _ in range(3)],
+        grid=(steps,),
+        in_specs=specs,
+        out_specs=[wide] * 3 + [narrow] * 6,
+    )(*operands)
+
+
 def per_device(
     block_inputs, mixed_inputs, token_ids, target_ids, final_gain, out_weight, head_weight,
     out_master, out_first, out_second, head_master, head_first, head_second,
@@ -661,11 +713,16 @@
         target_ids,
         token_ids,
     )
-    return (
-        *adam_update(out_master, out_first, out_second, out_gradient.reshape(out_master.shape)),
-        *adam_update(head_master, head_first, head_second, head_gradient),
-        *adam_update(embed_master, embed_first, embed_second, embed_gradient),
+    shape = out_master.shape
+    flat = (OWNED, WIDTH)
+    results = adam(
+        (
+            (out_gradient, out_master.reshape(flat), out_first.reshape(flat), out_second.reshape(flat)),
+            (head_gradient, head_master, head_first, head_second),
+            (embed_gradient, embed_master, embed_first, embed_second),
+        )
     )
+    return (*(value.reshape(shape) for value in results[:3]), *results[3:])
 
 
 def solution(mesh):

time: 120 us -> 118 us (0.983)
  other arithmetic: 4.04 us -> 0 us
  Pallas kernels: 115 us -> 117 us
    sub x2 -> x0, other arithmetic: 4.04 us -> none  [adam_update(): master - learning_rate * (first_next / (jnp.sqrt(second_next) + adam_eps)...]
    pallas_call x0 -> x1, Pallas kernels: none -> 3.08 us  [adam(): pl.pallas_call(adam_kernel, out_shape=[jax.ShapeDtypeStruct(groups[k][0]....]
where the time goes in v4:
time: 118 us; the launch traced here: 117 us
  Pallas kernels  117 us (99%)
    pallas_call x1, Pallas kernels, gradients(): pl.pallas_call(kernel, out_shape=(jax.ShapeDtypeStruct((OWNED, WIDTH), f3...  114 us
    pallas_call x1, Pallas kernels, adam(): pl.pallas_call(adam_kernel, out_shape=[jax.ShapeDtypeStruct(groups[k][0]....  3.08 us

profile of v4, /device:TPU:7, one launch (start us, length us, event | category | flops | bytes accessed | tf_op | source)
XLA Modules:
  0.0 117.4 jit_solution(9848837985420303036)
XLA Ops:
  0.6 113.6 %shard_map.223 = (f32[64,2048]{1,0:T(8,128)}, f32[8,2048]{1,0:T(8,128)}, f32[8,2048]{1,0:T(8,128)}) custom-call(bf16[256,2048]{1,0:T(8,128)(2,1)} %bitcast.10, bf16[256,2048]{1,0:T(8,128)(2,1)} %bitcast.11, bf16[256,2048]{1,0:T(8,128)(2,1)} %head_hbm.1, bf16[2048,2048]{1,0:T(8,128)(2,1)} %bitcast.9, f32[2048]{0:T(1024)} %gain_in.1, s32[4,64]{1,0:T(4,128)} %target_ids.1, ...), custom_call_target="tpu_custom_call" | custom-call | tf_op jit(solution)/shard_map/pallas_call | solution.py:598
  114.3 3.1 %shard_map.224 = (f32[64,2048]{1,0:T(8,128)}, f32[64,2048]{1,0:T(8,128)}, f32[64,2048]{1,0:T(8,128)}, f32[8,2048]{1,0:T(8,128)}, f32[8,2048]{1,0:T(8,128)}, /*in...) custom-call(f32[64,2048]{1,0:T(8,128)} %get-tuple-element.21.refs_0_, ...), custom_call_target="tpu_custom_call" | custom-call | tf_op jit(solution)/shard_map/pallas_call | solution.py:693

commit v5 on v4

--- a/solution.py
+++ b/solution.py
@@ -426,22 +426,22 @@
         psum[:, cols] = total
         return carry
 
+    def embed_part(part):
+        rows_ = section * SLICE + lax.broadcasted_iota(jnp.int32, (SLICE, TOKENS), 0)
+        embed = jnp.zeros((SLICE, 256), f32)
+        for m in range(part * 4, part * 4 + 4):
+            marks = (idsb[m, :1, :] == rows_).astype(f32).astype(bf16)
+            embed += jnp.dot(marks, bcot[m], preferred_element_type=f32)
+        return embed.reshape(REPLICAS, 8, 256)
+
     cotangent_part(0)
     lax.fori_loop(0, WIDTH // 256, near_product, 0)
     pass_diag(3)
-    for copy in core_z + core_diag:
-        copy.wait_recv()
     for copy in ids_sends:
         copy.wait_recv()
+    tile_e[...] = embed_part(0)
     cotangent_part(1)
-
-    rows_ = section * SLICE + lax.broadcasted_iota(jnp.int32, (SLICE, TOKENS), 0)
-    embed = jnp.zeros((SLICE, 256), f32)
-    for m in range(8):
-        marks = (idsb[m, :1, :] == rows_).astype(f32).astype(bf16)
-        embed += jnp.dot(marks, bcot[m], preferred_element_type=f32)
-    tile_e[...] = embed.reshape(REPLICAS, 8, 256)
-
+    tile_e[...] += embed_part(1)
     def send_embed(k, carry):
         target = (replica + k) % REPLICAS
         remote(
@@ -451,6 +451,9 @@
 
     lax.fori_loop(1, REPLICAS, send_embed, 0)
     pltpu.make_async_copy(tile_e.at[replica], er.at[replica], erv.at[0]).start()
+
+    for copy in core_z + core_diag:
+        copy.wait_recv()
 
     def product(n, carry):
         cols = pl.ds(pl.multiple_of(n * 256, 256), 256)

time: 118 us -> 117 us (level)
  Pallas kernels: 117 us -> 115 us
    pallas_call x1, Pallas kernels: 114 us -> 112 us  [gradients(): pl.pallas_call(kernel, out_shape=(jax.ShapeDtypeStruct((OWNED, WIDTH), f3...]
where the time goes in v5:
time: 117 us; the launch traced here: 116 us
  Pallas kernels  115 us (98%)
    pallas_call x1, Pallas kernels, gradients(): pl.pallas_call(kernel, out_shape=(jax.ShapeDtypeStruct((OWNED, WIDTH), f3...  112 us
    pallas_call x1, Pallas kernels, adam(): pl.pallas_call(adam_kernel, out_shape=[jax.ShapeDtypeStruct(groups[k][0]....  3.08 us

profile of v5, /device:TPU:7, one launch (start us, length us, event | category | flops | bytes accessed | tf_op | source)
XLA Modules:
  0.0 115.6 jit_solution(9603171639778626129)
XLA Ops:
  0.6 111.9 %shard_map.223 = (f32[64,2048]{1,0:T(8,128)}, f32[8,2048]{1,0:T(8,128)}, f32[8,2048]{1,0:T(8,128)}) custom-call(bf16[256,2048]{1,0:T(8,128)(2,1)} %bitcast.10, bf16[256,2048]{1,0:T(8,128)(2,1)} %bitcast.11, bf16[256,2048]{1,0:T(8,128)(2,1)} %head_hbm.1, bf16[2048,2048]{1,0:T(8,128)(2,1)} %bitcast.9, f32[2048]{0:T(1024)} %gain_in.1, s32[4,64]{1,0:T(4,128)} %target_ids.1, ...), custom_call_target="tpu_custom_call" | custom-call | tf_op jit(solution)/shard_map/pallas_call | solution.py:601
  112.5 3.1 %shard_map.224 = (f32[64,2048]{1,0:T(8,128)}, f32[64,2048]{1,0:T(8,128)}, f32[64,2048]{1,0:T(8,128)}, f32[8,2048]{1,0:T(8,128)}, f32[8,2048]{1,0:T(8,128)}, /*in...) custom-call(f32[64,2048]{1,0:T(8,128)} %get-tuple-element.21.refs_0_, ...), custom_call_target="tpu_custom_call" | custom-call | tf_op jit(solution)/shard_map/pallas_call | solution.py:696
